TPU v7x, 32 devices: a whole 2x2x4 slice. The times are simulated.
32 devices in a mesh: rep: 4 (over z), px: 4 (over x, core), py: 2 (over y).
Axes of the slice: x: 2, y: 2, z: 4, core: 2. Of those that a mesh axis runs over, the one named last changes fastest.
Arguments:
- state: float32 [12, 2, 192, 96, 256], P('rep', None, 'px', 'py'), parts along dimension 0, may hold values from -6 to 6
- cotangent: float32 [12, 2, 192, 96, 256], P('rep', None, 'px', 'py'), parts along dimension 0, may hold values from -6 to 6
- w_in: bfloat16 [512, 192], replicated, may hold values from -0.4375 to 0.4375
- b_in: float32 [512], replicated, may hold values from -5 to 5
- w_out: bfloat16 [192, 512], replicated, may hold values from -0.25 to 0.25
Outputs:
- state_grad: float32 [12, 2, 192, 96, 256], P('rep', None, 'px', 'py'), parts along dimension 0
- grad_in: float32 [512, 768], P(('px', 'py'), 'rep'), parts along dimension 1
- grad_out: float32 [768, 512], P('rep', ('px', 'py')), parts along dimension 0
- grad_bias: float32 [4, 512], P('rep', ('px', 'py')), parts along dimension 0
There are 4 independent parts, one for each index of `rep`. A program takes and returns all parts, laid end to end along the dimension named above; an argument that names none is the same for every part. Nothing has to cross between parts.
All inputs are finite; a program needn't handle non-finite values.
Results may differ from a plain program's by a relative error of at most 0.0065.
The roundings to bfloat16 on the way count: a program that leaves them out, or rounds other values in their place, can miss the bound.
Values may be sent and summed in bfloat16 or wider, within the bound.
A program may use at most 448 MiB of HBM per device.

v0:
```python
import math

import jax
import jax.numpy as jnp
from jax import lax
from jax.sharding import PartitionSpec as P

PATCH = 4


NU_DT = 5e-05
TIME_STEP = 0.01
FORCING = 20.0


def angles(leading, trailing, length):
    product = leading[:, None] * trailing[None, :] % length
    phases = product.astype(jnp.float32) * (2.0 * math.pi / length)
    factor = 1.0 / math.sqrt(length)
    return (jnp.cos(phases) * factor, jnp.sin(phases) * factor)


def mode_ids(count, length):
    counter = jnp.arange(count, dtype=jnp.int32)
    return jnp.where(counter < count // 2, counter, counter + length - count)


def mode_table(modes, length, direction):
    cosine, sine_part = angles(modes, jnp.arange(length, dtype=jnp.int32), length)
    top_rows = jnp.stack([cosine, direction * sine_part], axis=1)
    low_rows = jnp.stack([-direction * sine_part, cosine], axis=1)
    return jnp.stack([top_rows, low_rows], axis=0).astype(jnp.bfloat16)


def complex_table(length, direction):
    return mode_table(jnp.arange(length, dtype=jnp.int32), length, direction)


def real_table(length, mode_count):
    cosine, sine_part = angles(
        jnp.arange(mode_count, dtype=jnp.int32), jnp.arange(length, dtype=jnp.int32), length
    )
    return jnp.stack([cosine, -sine_part], axis=0).astype(jnp.bfloat16)


def box_order(length, span):
    counter = jnp.arange(length, dtype=jnp.int32)
    local = counter % span
    rows = span // PATCH
    return counter - local + local % rows * PATCH + local // rows


def signed(counter, length):
    return jnp.where(counter < length // 2, counter, counter - length).astype(jnp.float32)


def factors(ky_ids, kz_ids, length, ky_count):
    cutoff = length // 3
    wave_y = signed(ky_ids, ky_count)[:, None, None]
    wave_z = kz_ids.astype(jnp.float32)[None, :, None]
    wave_x = signed(jnp.arange(length, dtype=jnp.int32), length)[None, None, :]
    retained = (
        (jnp.abs(wave_x) <= cutoff) & (jnp.abs(wave_y) <= cutoff) & (wave_z <= cutoff)
    ).astype(jnp.float32)
    square = wave_x * wave_x + wave_y * wave_y + wave_z * wave_z
    damping = jnp.exp(-NU_DT * square)
    weight = jnp.where(kz_ids[None, :, None] == 0, 1.0, 2.0).astype(jnp.float32)
    return ((wave_x, wave_y, wave_z), retained, damping, weight, square)


def cross(former, latter):
    return [
        former[1] * latter[2] - former[2] * latter[1],
        former[2] * latter[0] - former[0] * latter[2],
        former[0] * latter[1] - former[1] * latter[0],
    ]


def curl_modes(waves, spectra):
    real_part = cross(waves, [spectra[slot, 0] for slot in range(3)])
    imag_part = cross(waves, [spectra[slot, 1] for slot in range(3)])
    return jnp.stack([jnp.stack([-imag_part[slot], real_part[slot]]) for slot in range(3)])


def project(waves, square, spectra):
    dotted = waves[0] * spectra[0] + waves[1] * spectra[1] + waves[2] * spectra[2]
    along_k = dotted / jnp.maximum(square, 1.0)
    return jnp.stack([spectra[slot] - waves[slot] * along_k for slot in range(3)])


def to_physical(spectra):
    channels, paired, width_y, width_z, length = spectra.shape
    parts_x = lax.axis_size("px")
    parts_y = lax.axis_size("py")
    order_y = box_order(length, length)
    order_z = box_order(length, length)
    inverse = complex_table(length, 1.0)
    y_table = mode_table(mode_ids(width_y * parts_x, length), length, 1.0)[..., order_y].reshape(
        2, parts_x, width_y, 2, length
    )
    z_table = real_table(length, width_z * parts_y)[..., order_z].reshape(
        2, parts_y, width_z, length
    )
    flat = spectra.astype(jnp.bfloat16).reshape(channels, paired, width_y * width_z, length)
    along_x = jnp.einsum(
        "crpn,rnsx->csxp", flat, inverse, preferred_element_type=jnp.float32
    ).astype(jnp.bfloat16)
    along_x = along_x.reshape(channels, 2, length, 1, width_y * width_z)
    moved = lax.all_to_all(along_x, ("px", "py"), split_axis=2, concat_axis=3, tiled=True)
    blocks = moved.reshape(moved.shape[0], 2, moved.shape[2], parts_x, parts_y, width_y, width_z)
    along_y = jnp.einsum(
        "csxjlam,sjaty->cxtlmy", blocks, y_table, preferred_element_type=jnp.float32
    ).astype(jnp.bfloat16)
    return jnp.einsum(
        "cxtlmy,tlmz->cxyz", along_y, z_table, preferred_element_type=jnp.float32
    ).astype(jnp.bfloat16)


def to_spectral(field, ky_count, mode_count):
    channels, span_x, span_y, length = field.shape
    parts_x = lax.axis_size("px")
    parts_y = lax.axis_size("py")
    width_y = ky_count // parts_x
    width_z = mode_count // parts_y
    order_y = box_order(length, span_y)
    order_z = box_order(length, length)
    forward = complex_table(length, -1.0)
    y_table = (
        mode_table(mode_ids(ky_count, length), length, -1.0)
        .transpose(0, 3, 2, 1)[:, order_y]
        .reshape(2, length, 2, parts_x, width_y)
    )
    z_table = real_table(length, mode_count)[..., order_z].reshape(2, parts_y, width_z, length)
    along_z = jnp.einsum(
        "cxyz,rlmz->crlmxy", field, z_table, preferred_element_type=jnp.float32
    ).astype(jnp.bfloat16)
    along_y = jnp.einsum(
        "crlmxy,rysja->csxjlam", along_z, y_table, preferred_element_type=jnp.float32
    ).astype(jnp.bfloat16)
    along_y = along_y.reshape(channels, 2, span_x, parts_x * parts_y, width_y * width_z)
    moved = lax.all_to_all(along_y, ("px", "py"), split_axis=3, concat_axis=2, tiled=True)
    number = moved.shape[0]
    flat = moved.reshape(number, 2, length, -1)
    along_x = jnp.einsum("csxp,sxtn->ctpn", flat, forward, preferred_element_type=jnp.float32)
    return along_x.reshape(number, 2, width_y, width_z, length)


def to_boxes(field):
    channels, span_x, span_y, span_z = field.shape
    tiles = field.reshape(
        channels, span_x // PATCH, PATCH, PATCH, span_y // PATCH, PATCH, span_z // PATCH
    )
    return tiles.transpose(0, 2, 3, 5, 1, 4, 6).reshape(channels * PATCH**3, -1)


def from_boxes(box_values, layout):
    channels, span_x, span_y, span_z = layout
    tiles = box_values.reshape(
        channels, PATCH, PATCH, PATCH, span_x // PATCH, span_y // PATCH, span_z // PATCH
    )
    return tiles.transpose(0, 4, 1, 2, 5, 3, 6).reshape(layout)


def closure_terms(velocity, force_adj, w_in, b_in, w_out):
    features = to_boxes(velocity)
    adjoints = to_boxes(force_adj)
    pre_act = jnp.dot(w_in, features, preferred_element_type=jnp.float32) + b_in[:, None]
    hidden = jax.nn.silu(pre_act).astype(jnp.bfloat16)
    sigmoid = jax.nn.sigmoid(pre_act)
    hidden_adj = FORCING * jnp.dot(w_out.T, adjoints, preferred_element_type=jnp.float32)
    pre_adj = (hidden_adj * sigmoid * (1.0 + pre_act * (1.0 - sigmoid))).astype(jnp.bfloat16)
    grad_in = jnp.dot(pre_adj, features.T, preferred_element_type=jnp.float32)
    grad_out = FORCING * jnp.dot(adjoints, hidden.T, preferred_element_type=jnp.float32)
    grad_bias = jnp.sum(pre_adj.astype(jnp.float32), axis=1)[None, :]
    feat_adj = jnp.dot(w_in.T, pre_adj, preferred_element_type=jnp.float32).astype(jnp.bfloat16)
    feat_adj = lax.optimization_barrier(from_boxes(feat_adj, velocity.shape))
    return (feat_adj, grad_in, grad_out, grad_bias)


def field_cross(former, latter):
    return cross(
        [former[slot].astype(jnp.float32) for slot in range(3)],
        [latter[slot].astype(jnp.float32) for slot in range(3)],
    )


def shards(state, cotangent, w_in, b_in, w_out):
    width_y = state.shape[2]
    width_z = state.shape[3]
    length = state.shape[4]
    ky_count = width_y * lax.axis_size("px")
    ky_ids = lax.axis_index("px") * width_y + jnp.arange(width_y, dtype=jnp.int32)
    kz_ids = lax.axis_index("py") * width_z + jnp.arange(width_z, dtype=jnp.int32)
    waves, retained, damping, weight, square = factors(ky_ids, kz_ids, length, ky_count)
    kept = retained * state
    force_spec = TIME_STEP * retained * project(waves, square, damping * cotangent)
    modes = width_z * lax.axis_size("py")
    force_adj = to_physical(force_spec)
    velocity = to_physical(weight * kept)
    vorticity = to_physical(weight * curl_modes(waves, kept))
    vort_adj = jnp.stack(field_cross(force_adj, velocity)).astype(jnp.bfloat16)
    spec_vort = to_spectral(vort_adj, ky_count, modes)
    feat_adj, grad_in, grad_out, grad_bias = closure_terms(velocity, force_adj, w_in, b_in, w_out)
    turned = field_cross(vorticity, force_adj)
    vel_adj = jnp.stack([feat_adj[slot].astype(jnp.float32) + turned[slot] for slot in range(3)])
    spec_vel = to_spectral(vel_adj.astype(jnp.bfloat16), ky_count, modes)
    state_grad = damping * cotangent + weight * retained * (
        spec_vel + curl_modes(waves, spec_vort)
    )
    grad_in, grad_out, grad_bias = (
        lax.psum_scatter(grad_in, ("px", "py"), scatter_dimension=0, tiled=True),
        lax.psum_scatter(grad_out, ("px", "py"), scatter_dimension=1, tiled=True),
        lax.psum_scatter(grad_bias, ("px", "py"), scatter_dimension=1, tiled=True),
    )
    return (state_grad, grad_in, grad_out, grad_bias)


def solution(mesh):
    return jax.shard_map(
        shards,
        mesh=mesh,
        in_specs=(
            P("rep", None, "px", "py", None),
            P("rep", None, "px", "py", None),
            P(),
            P(),
            P(),
        ),
        out_specs=(
            P("rep", None, "px", "py", None),
            P(("px", "py"), "rep"),
            P("rep", ("px", "py")),
            P("rep", ("px", "py")),
        ),
        check_vma=False,
    )
```

profile of v0, /device:TPU:0, one launch (start us, length us, event | category | flops | bytes accessed | tf_op | source)
XLA Modules:
  0.0 1128.6 jit_solution(6317094853116231177)
XLA Ops:
  26.0 9.3 multiply_subtract_fusion.1
  39.0 7.2 fusion.75
  46.3 23.6 %copy.174 = bf16[3,2,256,1,2304]{4,1,3,0,2:T(2,128)(2,1)} copy(bf16[3,2,256,1,2304]{4,2,0,1,3:T(8,128)(2,1)S(1)} %fusion.75) | data formatting | bytes 14155776 | tf_op jit(solution)/shard_map/reshape | solution.py:108
  69.9 16.6 %all-to-all-start = ((bf16[3,2,256,1,2304]{4,1,3,0,2:T(2,128)(2,1)}), bf16[3,2,256,1,2304]{4,1,3,0,2:T(2,128)(2,1)}, u32[]{:S(2)}, u32[]{:S(2)}) async-start(bf16[3,2,256,1,2304]{4,1,3,0,2:T(2,128)(2,1)} %copy.174), calls=%async_computation | async-start | bytes 14155776 | tf_op jit(solution)/shard_map/all_to_all | solution.py:109
  86.9 12.8 %multiply_convert_fusion = (bf16[3,2,48,48,256]{4,3,2,1,0:T(8,128)(2,1)S(1)}, f32[3,2,48,48,256]{4,3,2,1,0:T(8,128)}) fusion(f32[48]{0:T(128)S(1)} %copy-done.28, f32[3,2,48,48,256]{4,3,2,1,0:T(8,128)} %param.5, f32[48,48,256]{2,1,0:T(8,128)S(1)} %and_convert_fusion), kind=kLoop, calls=%fused_computation.59 | loop fusion | flops 10616832 | bytes 37748928 | tf_op jit(solution)/shard_map/convert_element_type | solution.py:104
  105.6 27.6 %copy.180 = bf16[3,2,256,1,2304]{4,1,3,0,2:T(2,128)(2,1)} copy(bf16[3,2,256,1,2304]{4,2,0,1,3:T(8,128)(2,1)} %fusion.74) | data formatting | bytes 14155776 | tf_op jit(solution)/shard_map/reshape | solution.py:108
  133.2 33.0 %all-to-all-done = bf16[3,2,256,1,2304]{4,1,3,0,2:T(2,128)(2,1)} async-done(((bf16[3,2,256,1,2304]{4,1,3,0,2:T(2,128)(2,1)}), bf16[3,2,256,1,2304]{4,1,3,0,2:T(2,128)(2,1)}, u32[]{:S(2)}, u32[]{:S(2)}) %all-to-all-start) | async-done | bytes 7077920 | tf_op jit(solution)/shard_map/all_to_all | solution.py:109
  181.0 9.7 fusion.155
  204.4 24.0 %copy.187 = bf16[3,2,256,1,2304]{4,1,3,0,2:T(2,128)(2,1)} copy(bf16[3,2,256,1,2304]{4,2,0,1,3:T(8,128)(2,1)S(1)} %fusion.78) | data formatting | bytes 14155776 | tf_op jit(solution)/shard_map/reshape | solution.py:108
  230.2 9.8 copy.331
  240.1 28.9 %reshape.1131 = bf16[3,2,32,4,2,48,48]{6,5,4,3,2,1,0:T(8,128)(2,1)} reshape(bf16[3,2,32,8,1,2304]{5,3,2,1,0,4:T(8,128)(2,1)} %bitcast.414) | data formatting | bytes 14155776 | tf_op jit(solution)/shard_map/reshape | solution.py:110
  273.9 9.8 copy.330
  283.7 29.0 %reshape.1136 = bf16[3,2,32,4,2,48,48]{6,5,4,3,2,1,0:T(8,128)(2,1)} reshape(bf16[3,2,32,8,1,2304]{5,3,2,1,0,4:T(8,128)(2,1)} %bitcast.415) | data formatting | bytes 14155776 | tf_op jit(solution)/shard_map/reshape | solution.py:110
  312.7 16.2 %bitcast_convert_fusion.3 = bf16[3,32,256,256]{3,2,1,0:T(8,128)(2,1)} fusion(bf16[2,4,48,2,256,1,1,1]{4,2,1,3,0,7,6,5:T(8,128)(2,1)S(1)} %bitcast.429, bf16[2,2,48,256,1,1]{3,2,1,0,5,4:T(8,128)(2,1)S(1)} %bitcast.432, bf16[3,2,32,4,2,48,48]{6,5,4,3,2,1,0:T(8,128)(2,1)} %reshape.1136), kind=kOutput, calls=%fused_computation.21 | convolution fusion | flops 6050807808 | bytes 20152320 | tf_op jit(solution)/shard_map/cxtlmy,tlmz->cxyz/dot_general | solution.py:114
  328.9 36.2 %reshape.1137 = bf16[3,8,4,4,64,4,64]{6,5,4,3,2,1,0:T(4,128)(2,1)} reshape(bf16[3,32,256,256]{3,2,1,0:T(8,128)(2,1)} %bitcast_convert_fusion.3) | data formatting | bytes 25165824 | tf_op jit(solution)/shard_map/reshape | solution.py:150
  365.0 16.4 %bitcast_convert_fusion.4 = bf16[3,32,256,256]{3,2,1,0:T(8,128)(2,1)} fusion(bf16[2,4,48,2,256,1,1,1]{4,2,1,3,0,7,6,5:T(8,128)(2,1)S(1)} %bitcast.430, bf16[2,2,48,256,1,1]{3,2,1,0,5,4:T(8,128)(2,1)S(1)} %bitcast.433, bf16[3,2,32,4,2,48,48]{6,5,4,3,2,1,0:T(8,128)(2,1)} %reshape.1131), kind=kOutput, calls=%fused_computation.22 | convolution fusion | flops 6050807808 | bytes 20152320 | tf_op jit(solution)/shard_map/cxtlmy,tlmz->cxyz/dot_general | solution.py:114
  381.4 36.2 %reshape.1132 = bf16[3,8,4,4,64,4,64]{6,5,4,3,2,1,0:T(4,128)(2,1)} reshape(bf16[3,32,256,256]{3,2,1,0:T(8,128)(2,1)} %bitcast_convert_fusion.4) | data formatting | bytes 25165824 | tf_op jit(solution)/shard_map/reshape | solution.py:150
  417.6 11.3 %fusion.49 = (bf16[1,32,256,256]{3,2,1,0:T(8,128)(2,1)S(1)}, bf16[1,32,256,256]{3,2,1,0:T(8,128)(2,1)S(1)}, bf16[1,32,256,256]{3,2,1,0:T(8,128)(2,1)S(1)}) fusion(bf16[3,32,256,256]{3,2,1,0:T(8,128)(2,1)} %bitcast_convert_fusion.3, bf16[3,32,256,256]{3,2,1,0:T(8,128)(2,1)} %bitcast_convert_fusion.4), kind=kLoop, calls=%fused_computation.86 | loop fusion | flops 37748736 | bytes 37748736 | tf_op jit(solution)/shard_map/convert
  435.4 15.6 %fusion.11 = bf16[3,2,32,4,2,48,48]{6,5,2,4,0,3,1:T(8,128)(2,1)} fusion(bf16[2,2,48,3,32,256]{5,2,0,4,1,3:T(8,128)(2,1)} %fusion.27, bf16[2,256,2,4,48,1,1,1]{1,4,3,2,0,7,6,5:T(8,128)(2,1)} %bitcast.427), kind=kOutput, calls=%fused_computation.27 | convolution fusion | flops 3627417600 | bytes 16908288 | tf_op jit(solution)/shard_map/crlmxy,rysja->csxjlam/dot_general | solution.py:137
  451.0 18.1 %copy.270 = bf16[3,2,32,4,2,48,48]{6,5,2,1,0,4,3:T(8,128)(2,1)} copy(bf16[3,2,32,4,2,48,48]{6,5,2,4,0,3,1:T(8,128)(2,1)} %fusion.11) | data formatting | bytes 14155776 | tf_op jit(solution)/shard_map/reshape | solution.py:140
  469.1 26.4 %reshape.1212 = bf16[3,2,32,8,2304]{4,2,1,0,3:T(8,128)(2,1)} reshape(bf16[3,2,32,4,2,48,48]{6,5,2,1,0,4,3:T(8,128)(2,1)} %copy.270) | data formatting | bytes 14155776 | tf_op jit(solution)/shard_map/reshape | solution.py:140
  495.5 22.6 %copy.327 = bf16[3,8,4,4,64,4,64]{6,4,1,5,3,2,0:T(8,128)(2,1)} copy(bf16[3,8,4,4,64,4,64]{6,5,4,3,2,1,0:T(4,128)(2,1)} %reshape.1137) | data formatting | bytes 25165824 | tf_op jit(solution)/shard_map/reshape | solution.py:150
  518.2 29.1 %reshape.1138 = bf16[192,32768]{1,0:T(8,128)(2,1)} reshape(bf16[3,4,4,4,8,64,64]{6,5,4,3,2,1,0:T(8,128)(2,1)} %bitcast.405) | data formatting | bytes 25165824 | tf_op jit(solution)/shard_map/reshape | solution.py:153
  552.1 9.8 copy.329
  562.0 29.2 %reshape.1142 = bf16[3,2,32,4,2,48,48]{6,5,4,3,2,1,0:T(8,128)(2,1)} reshape(bf16[3,2,32,8,1,2304]{5,3,2,1,0,4:T(8,128)(2,1)} %bitcast.416) | data formatting | bytes 14155776 | tf_op jit(solution)/shard_map/reshape | solution.py:110
  591.1 16.2 %bitcast_convert_fusion.2 = bf16[3,32,256,256]{3,2,1,0:T(8,128)(2,1)} fusion(bf16[2,4,48,2,256,1,1,1]{4,2,1,3,0,7,6,5:T(8,128)(2,1)S(1)} %bitcast.431, bf16[2,2,48,256,1,1]{3,2,1,0,5,4:T(8,128)(2,1)S(1)} %bitcast.435, bf16[3,2,32,4,2,48,48]{6,5,4,3,2,1,0:T(8,128)(2,1)} %reshape.1142), kind=kOutput, calls=%fused_computation.20 | convolution fusion | flops 6050807808 | bytes 20152320 | tf_op jit(solution)/shard_map/cxtlmy,tlmz->cxyz/dot_general | solution.py:114
  607.3 22.6 %copy.328 = bf16[3,8,4,4,64,4,64]{6,4,1,5,3,2,0:T(8,128)(2,1)} copy(bf16[3,8,4,4,64,4,64]{6,5,4,3,2,1,0:T(4,128)(2,1)} %reshape.1132) | data formatting | bytes 25165824 | tf_op jit(solution)/shard_map/reshape | solution.py:150
  629.9 29.1 %reshape.1133 = bf16[192,32768]{1,0:T(8,128)(2,1)} reshape(bf16[3,4,4,4,8,64,64]{6,5,4,3,2,1,0:T(8,128)(2,1)} %bitcast.406) | data formatting | bytes 25165824 | tf_op jit(solution)/shard_map/reshape | solution.py:153
  659.0 27.8 %fusion.156 = f32[32768,512]{1,0:T(8,128)} fusion(bf16[192,32768]{1,0:T(8,128)(2,1)} %reshape.1138, bf16[512,192]{0,1:T(8,128)(2,1)S(1)} %copy-done), kind=kOutput, calls=%fused_computation.263 | convolution fusion | flops 6442450944 | bytes 79888384 | tf_op jit(solution)/shard_map/dot_general | solution.py:167
  686.8 46.9 %convert_reduce_fusion = (f32[512]{0:T(512)S(1)}, bf16[512,32768]{0,1:T(8,128)(2,1)}) fusion(f32[32768,512]{1,0:T(8,128)} %fusion.156, f32[512]{0:T(512)S(1)} %copy-done.32, bf16[192,32768]{1,0:T(8,128)(2,1)} %reshape.1133, bf16[192,512]{1,0:T(8,128)(2,1)S(1)} %copy-done.31), kind=kOutput, calls=%fused_computation.14 | convolution fusion | flops 6660554240 | bytes 113446912 | tf_op jit(solution)/shard_map/dot_general | solution.py:170
  734.7 21.2 %fusion.7 = bf16[192,32768]{1,0:T(8,128)(2,1)} fusion(bf16[512,32768]{0,1:T(8,128)(2,1)} %get-tuple-element.59, bf16[512,192]{0,1:T(8,128)(2,1)S(1)} %copy-done), kind=kOutput, calls=%fused_computation.16 | convolution fusion | flops 6448742400 | bytes 46333952 | tf_op jit(solution)/shard_map/dot_general | solution.py:175
  755.8 30.9 %reshape.1139 = bf16[3,4,4,4,8,64,64]{6,5,4,3,2,1,0:T(8,128)(2,1)} reshape(bf16[192,32768]{1,0:T(8,128)(2,1)} %fusion.7) | data formatting | bytes 25165824 | tf_op jit(solution)/shard_map/reshape | solution.py:158
  786.7 29.0 %copy.326 = bf16[3,4,4,4,8,64,64]{6,3,5,2,1,4,0:T(4,128)(2,1)} copy(bf16[3,4,4,4,8,64,64]{6,5,4,3,2,1,0:T(8,128)(2,1)} %reshape.1139) | data formatting | bytes 25165824 | tf_op jit(solution)/shard_map/reshape | solution.py:158
  815.7 35.7 %reshape.1140 = bf16[3,32,256,256]{3,2,1,0:T(8,128)(2,1)} reshape(bf16[3,8,4,4,64,4,64]{6,5,4,3,2,1,0:T(4,128)(2,1)} %bitcast.407) | data formatting | bytes 25165824 | tf_op jit(solution)/shard_map/reshape | solution.py:161
  851.4 18.5 %fusion.44 = (bf16[1,32,256,256]{3,2,1,0:T(8,128)(2,1)}, bf16[1,32,256,256]{3,2,1,0:T(8,128)(2,1)}, bf16[1,32,256,256]{3,2,1,0:T(8,128)(2,1)}) fusion(bf16[3,32,256,256]{3,2,1,0:T(8,128)(2,1)} %reshape.1140, bf16[3,32,256,256]{3,2,1,0:T(8,128)(2,1)} %bitcast_convert_fusion.2, bf16[3,32,256,256]{3,2,1,0:T(8,128)(2,1)} %bitcast_convert_fusion.4), kind=kLoop, calls=%fused_computation.81 | loop fusion | flops 50331648 | bytes 50331648 | tf_op jit(solution)/shard_map/convert.3
  870.0 9.6 fusion.22
  879.6 39.9 %fusion.10 = bf16[3,2,32,4,2,48,48]{6,5,2,4,0,3,1:T(8,128)(2,1)} fusion(bf16[2,2,48,3,32,256]{5,2,0,4,1,3:T(8,128)(2,1)} %fusion.22, bf16[2,256,2,4,48,1,1,1]{1,4,3,2,0,7,6,5:T(8,128)(2,1)S(1)} %bitcast.428), kind=kOutput, calls=%fused_computation.26 | convolution fusion | flops 3627417600 | bytes 16908288 | tf_op jit(solution)/shard_map/crlmxy,rysja->csxjlam/dot_general | solution.py:137
  919.5 15.4 %fusion.157 = f32[512,192]{1,0:T(8,128)} fusion(bf16[512,32768]{0,1:T(8,128)(2,1)} %get-tuple-element.59, bf16[192,32768]{1,0:T(8,128)(2,1)S(1)} %bitcast.413), kind=kOutput, calls=%fused_computation.264 | convolution fusion | flops 6442450944 | bytes 46530560 | tf_op jit(solution)/shard_map/dot_general | solution.py:172
  934.9 18.2 %copy.263 = bf16[3,2,32,4,2,48,48]{6,5,2,1,0,4,3:T(8,128)(2,1)} copy(bf16[3,2,32,4,2,48,48]{6,5,2,4,0,3,1:T(8,128)(2,1)} %fusion.10) | data formatting | bytes 14155776 | tf_op jit(solution)/shard_map/reshape | solution.py:140
  953.0 26.2 %reshape.1211 = bf16[3,2,32,8,2304]{4,2,1,0,3:T(8,128)(2,1)} reshape(bf16[3,2,32,4,2,48,48]{6,5,2,1,0,4,3:T(8,128)(2,1)} %copy.263) | data formatting | bytes 14155776 | tf_op jit(solution)/shard_map/reshape | solution.py:140
  984.2 31.2 %fusion.92 = f32[192,512]{0,1:T(8,128)} fusion(bf16[192,32768]{1,0:T(8,128)(2,1)} %reshape.1133, f32[32768,512]{1,0:T(8,128)} %fusion.156, f32[512]{0:T(512)S(1)} %copy-done.32), kind=kOutput, calls=%fused_computation.154 | convolution fusion | flops 6543212544 | bytes 80087040 | tf_op jit(solution)/shard_map/dot_general | solution.py:173
  1020.5 7.4 convolution_bitcast_fusion
  1027.9 15.3 %copy.205 = f32[3,2,2304,256]{3,2,1,0:T(8,128)} copy(f32[3,2,2304,256]{2,3,0,1:T(8,128)} %convolution_bitcast_fusion) | data formatting | bytes 28311552 | tf_op jit(solution)/shard_map/csxp,sxtn->ctpn/transpose | solution.py:144
  1043.2 10.4 subtract_negate_fusion.1
  1053.7 13.9 %all-to-all-done.3 = bf16[3,2,32,8,2304]{4,2,1,0,3:T(8,128)(2,1)} async-done(((bf16[3,2,32,8,2304]{4,2,1,0,3:T(8,128)(2,1)}), bf16[3,2,32,8,2304]{4,2,1,0,3:T(8,128)(2,1)}, u32[]{:S(2)}, u32[]{:S(2)}) %all-to-all-start.3) | async-done | bytes 7077920 | tf_op jit(solution)/shard_map/all_to_all | solution.py:141
  1071.2 7.4 convolution_bitcast_fusion.1
  1078.5 15.5 %copy.198 = f32[3,2,2304,256]{3,2,1,0:T(8,128)} copy(f32[3,2,2304,256]{2,3,0,1:T(8,128)} %convolution_bitcast_fusion.1) | data formatting | bytes 28311552 | tf_op jit(solution)/shard_map/csxp,sxtn->ctpn/transpose | solution.py:144
  1106.8 14.8 %fusion.21 = f32[3,2,48,48,256]{4,3,2,1,0:T(8,128)} fusion(f32[3,2,48,48,256]{4,3,2,1,0:T(8,128)S(1)} %bitcast.411, f32[1,2,48,48,256]{4,3,2,1,0:T(8,128)} %maximum_bitcast_fusion.6, f32[1,2,48,48,256]{4,3,2,1,0:T(8,128)S(1)} %maximum_bitcast_fusion.5, f32[1,2,48,48,256]{4,3,2,1,0:T(8,128)} %maximum_bitcast_fusion.4, f32[48,48,256]{2,1,0:T(8,128)} %and_select_fusion, ...), kind=kLoop, calls=%fused_computation.55 | loop fusion | flops 21233664 | bytes 61341696 | tf_op jit(solution)/shard_map/add | solution.py:207
  (153 shorter events, 102.5 us)
Async XLA Ops:
  7.2 651.8 %copy-start = (bf16[512,192]{0,1:T(8,128)(2,1)S(1)}, bf16[512,192]{0,1:T(8,128)(2,1)}, u32[]{:S(2)}) copy-start(bf16[512,192]{0,1:T(8,128)(2,1)} %param.7) | copy-start | bytes 589828
  8.3 12.4 %copy-start.29 = (pred[48]{0:T(512)(128)(4,1)}, pred[48]{0:T(512)(128)(4,1)S(1)}, u32[]{:S(2)}) copy-start(pred[48]{0:T(512)(128)(4,1)S(1)} %broadcast_compare_fusion) | copy-start | bytes 148
  8.9 162.3 %copy-start.20 = (f32[48]{0:T(128)}, f32[48]{0:T(128)S(1)}, u32[]{:S(2)}) copy-start(f32[48]{0:T(128)S(1)} %get-tuple-element.68) | copy-start | bytes 580
  13.8 6.9 copy-start.2
  13.9 6.9 copy-start.22
  13.9 6.9 copy-start.25
  20.7 5.3 copy-start.1
  36.1 1.1 copy-start.16
  39.0 7.2 copy-start.12
  39.0 7.2 copy-start.14
  69.9 16.6 %copy-start.17 = (pred[48,256]{1,0:T(8,128)(4,1)S(1)}, pred[48,256]{1,0:T(8,128)(4,1)}, u32[]{:S(2)}) copy-start(pred[48,256]{1,0:T(8,128)(4,1)} %copy-done.16) | copy-start | bytes 36868
  69.9 16.6 %copy-start.30 = (pred[48]{0:T(512)(128)(4,1)S(1)}, pred[48]{0:T(512)(128)(4,1)}, u32[]{:S(2)}) copy-start(pred[48]{0:T(512)(128)(4,1)} %copy-done.29) | copy-start | bytes 148
  69.9 17.0 %copy-start.28 = (f32[48]{0:T(128)S(1)}, f32[48]{0:T(128)}, u32[]{:S(2)}) copy-start(f32[48]{0:T(128)} %get-tuple-element.60) | copy-start | bytes 580
  69.9 96.3 %all-to-all-start = ((bf16[3,2,256,1,2304]{4,1,3,0,2:T(2,128)(2,1)}), bf16[3,2,256,1,2304]{4,1,3,0,2:T(2,128)(2,1)}, u32[]{:S(2)}, u32[]{:S(2)}) async-start(bf16[3,2,256,1,2304]{4,1,3,0,2:T(2,128)(2,1)} %copy.174), calls=%async_computation | async-start | bytes 14155776 | tf_op jit(solution)/shard_map/all_to_all | solution.py:109
  86.9 12.8 %copy-start.13 = (bf16[1,256,2,256]{1,3,0,2:T(8,128)(2,1)S(1)}, bf16[1,256,2,256]{1,3,0,2:T(8,128)(2,1)}, u32[]{:S(2)}) copy-start(bf16[1,256,2,256]{1,3,0,2:T(8,128)(2,1)} %copy-done.12) | copy-start | bytes 786436
  86.9 12.8 %copy-start.15 = (bf16[1,256,2,256]{1,3,0,2:T(8,128)(2,1)S(1)}, bf16[1,256,2,256]{1,3,0,2:T(8,128)(2,1)}, u32[]{:S(2)}) copy-start(bf16[1,256,2,256]{1,3,0,2:T(8,128)(2,1)} %copy-done.14) | copy-start | bytes 786436
  133.2 38.1 %copy-start.23 = (f32[48]{0:T(128)S(1)}, f32[48]{0:T(128)}, u32[]{:S(2)}) copy-start(f32[48]{0:T(128)} %get-tuple-element.69) | copy-start | bytes 580
  166.2 102.8 %all-to-all-start.1 = ((bf16[3,2,256,1,2304]{4,1,3,0,2:T(2,128)(2,1)}), bf16[3,2,256,1,2304]{4,1,3,0,2:T(2,128)(2,1)}, u32[]{:S(2)}, u32[]{:S(2)}) async-start(bf16[3,2,256,1,2304]{4,1,3,0,2:T(2,128)(2,1)} %copy.180), calls=%async_computation.1 | async-start | bytes 14155776 | tf_op jit(solution)/shard_map/all_to_all | solution.py:109
  181.0 184.1 %copy-start.10 = (bf16[2,192,2,256]{3,1,2,0:T(8,128)(2,1)}, bf16[2,192,2,256]{3,1,2,0:T(8,128)(2,1)S(1)}, u32[]{:S(2)}) copy-start(bf16[2,192,2,256]{3,1,2,0:T(8,128)(2,1)S(1)} %copy.172) | copy-start | bytes 1179652
  181.0 9.7 copy-start.26
  269.0 278.2 %all-to-all-start.2 = ((bf16[3,2,256,1,2304]{4,1,3,0,2:T(2,128)(2,1)}), bf16[3,2,256,1,2304]{4,1,3,0,2:T(2,128)(2,1)}, u32[]{:S(2)}, u32[]{:S(2)}) async-start(bf16[3,2,256,1,2304]{4,1,3,0,2:T(2,128)(2,1)} %copy.187), calls=%async_computation.2 | async-start | bytes 14155776 | tf_op jit(solution)/shard_map/all_to_all | solution.py:109
  283.7 29.0 %copy-start.18 = (bf16[2,96,256]{2,1,0:T(8,128)(2,1)S(1)}, bf16[2,96,256]{2,1,0:T(8,128)(2,1)}, u32[]{:S(2)}) copy-start(bf16[2,96,256]{2,1,0:T(8,128)(2,1)} %copy.170) | copy-start | bytes 294916
  547.3 432.0 %all-to-all-start.4 = ((bf16[3,2,32,8,2304]{4,2,1,0,3:T(8,128)(2,1)}), bf16[3,2,32,8,2304]{4,2,1,0,3:T(8,128)(2,1)}, u32[]{:S(2)}, u32[]{:S(2)}) async-start(bf16[3,2,32,8,2304]{4,2,1,0,3:T(8,128)(2,1)} %reshape.1212), calls=%async_computation.4 | async-start | bytes 14155776 | tf_op jit(solution)/shard_map/all_to_all | solution.py:141
  552.1 463.4 %reduce-scatter.10.cloned.1.call-start = ((), (), s32[]{:S(2)}) async-start(), calls=%async_computation.10 | async-start | bytes 294912
  562.0 29.2 %copy-start.11 = (bf16[2,192,2,256]{3,1,2,0:T(8,128)(2,1)S(1)}, bf16[2,192,2,256]{3,1,2,0:T(8,128)(2,1)}, u32[]{:S(2)}) copy-start(bf16[2,192,2,256]{3,1,2,0:T(8,128)(2,1)} %copy-done.10) | copy-start | bytes 1179652
  659.0 27.8 %copy-start.31 = (bf16[192,512]{1,0:T(8,128)(2,1)S(1)}, bf16[192,512]{1,0:T(8,128)(2,1)}, u32[]{:S(2)}) copy-start(bf16[192,512]{1,0:T(8,128)(2,1)} %param.9) | copy-start | bytes 589828
  659.0 27.8 %copy-start.32 = (f32[512]{0:T(512)S(1)}, f32[512]{0:T(512)}, u32[]{:S(2)}) copy-start(f32[512]{0:T(512)} %param.8) | copy-start | bytes 6148
  734.6 387.0 %reduce-scatter.6.cloned.1.call-start = ((), (), s32[]{:S(2)}) async-start(), calls=%async_computation.8 | async-start | bytes 589824 | tf_op jit(solution)/shard_map/reduce_scatter | solution.py:211
  851.4 18.6 %copy-start.19 = (bf16[2,96,256]{2,1,0:T(8,128)(2,1)S(1)}, bf16[2,96,256]{2,1,0:T(8,128)(2,1)}, u32[]{:S(2)}) copy-start(bf16[2,96,256]{2,1,0:T(8,128)(2,1)} %copy.170) | copy-start | bytes 294916
  870.0 9.6 copy-start.9
  870.0 49.5 %slice-start.4 = ((s8[12582912]{0:T(1024)(128)(4,1)}), s8[4194304]{0:T(1024)(128)(4,1)S(1)}, s32[]{:S(2)}) async-start(s8[12582912]{0:T(1024)(128)(4,1)} %bitcast.412), calls=%async_computation.15 | async-start | bytes 8388608
  870.0 49.5 %slice-start.5 = ((s8[12582912]{0:T(1024)(128)(4,1)}), s8[4194304]{0:T(1024)(128)(4,1)S(1)}, s32[]{:S(2)}) async-start(s8[12582912]{0:T(1024)(128)(4,1)} %bitcast.412), calls=%async_computation.16 | async-start | bytes 8388608
  879.6 39.9 %slice-start.6 = ((s8[12582912]{0:T(1024)(128)(4,1)}), s8[4194304]{0:T(1024)(128)(4,1)S(1)}, s32[]{:S(2)}) async-start(s8[12582912]{0:T(1024)(128)(4,1)} %bitcast.412), calls=%async_computation.17 | async-start | bytes 8388608
  979.3 88.2 %all-to-all-start.3 = ((bf16[3,2,32,8,2304]{4,2,1,0,3:T(8,128)(2,1)}), bf16[3,2,32,8,2304]{4,2,1,0,3:T(8,128)(2,1)}, u32[]{:S(2)}, u32[]{:S(2)}) async-start(bf16[3,2,32,8,2304]{4,2,1,0,3:T(8,128)(2,1)} %reshape.1211), calls=%async_computation.3 | async-start | bytes 14155776 | tf_op jit(solution)/shard_map/all_to_all | solution.py:141
  984.2 137.4 %reduce-scatter.8.cloned.1.call-start = ((), (), s32[]{:S(2)}) async-start(), calls=%async_computation.9 | async-start | bytes 589824 | tf_op jit(solution)/shard_map/reduce_scatter | solution.py:212
  1016.8 3.7 copy-start.7
  1016.8 3.7 copy-start.8
  1027.9 15.3 %copy-start.21 = (f32[48]{0:T(128)S(1)}, f32[48]{0:T(128)}, u32[]{:S(2)}) copy-start(f32[48]{0:T(128)} %copy-done.20) | copy-start | bytes 580
  1027.9 15.3 %copy-start.24 = (f32[48]{0:T(128)S(1)}, f32[48]{0:T(128)}, u32[]{:S(2)}) copy-start(f32[48]{0:T(128)} %get-tuple-element.69) | copy-start | bytes 580
  1027.9 15.3 %copy-start.27 = (f32[256]{0:T(256)S(1)}, f32[256]{0:T(256)}, u32[]{:S(2)}) copy-start(f32[256]{0:T(256)} %fusion.140) | copy-start | bytes 3076
  1094.0 3.1 copy-start.5
  1094.0 3.8 copy-start.6
  1094.0 9.3 slice-start
  1094.0 10.3 slice-start.1
  1096.9 3.6 copy-start.4
  1097.8 7.8 slice-start.2
  1100.6 5.8 copy-start.3
  1100.6 6.2 slice-start.3
Sparse Core Ops, SparseCore 0:
  734.7 35.8 reduce-scatter.9
  979.4 41.3 reduce-scatter.5
  1024.5 36.3 reduce-scatter.7
where the time goes:
time: 1150 us; the launch traced here: 1130 us
  local copies, waits for them, and re-layouts  618 us (54%)
  matrix products  297 us (26%)
  other arithmetic  115 us (10%)
  waiting for transfers between devices  46.9 us (4%)
  starting transfers between devices  36 us (3%)
  between operations  14.9 us (1%)
    reshape x4, local copies, waits for them, and re-layouts, to_boxes(): field.reshape(channels, span_x // PATCH, PATCH, PATCH, span_y // PATCH, P...  118 us
    reshape x4, local copies, waits for them, and re-layouts, to_spectral(): along_y.reshape(channels, 2, span_x, parts_x * parts_y, width_y * width_z)  88.9 us
    reshape x3, local copies, waits for them, and re-layouts, to_physical(): moved.reshape(moved.shape[0], 2, moved.shape[2], parts_x, parts_y, width_...  87.1 us
    reshape x3, local copies, waits for them, and re-layouts, to_physical(): along_x = along_x.reshape(channels, 2, length, 1, width_y * width_z)  75.2 us
    reshape x2, local copies, waits for them, and re-layouts, from_boxes(): box_values.reshape(channels, PATCH, PATCH, PATCH, span_x // PATCH, span_y...  59.9 us
    reshape x2, local copies, waits for them, and re-layouts, to_boxes(): tiles.transpose(0, 2, 3, 5, 1, 4, 6).reshape(channels * PATCH ** 3, -1)  58.2 us
    dot_general x2, matrix products, to_spectral(): jnp.einsum('crlmxy,rysja->csxjlam', along_z, y_table, preferred_element_t...  55.5 us
    dot_general x3, matrix products, to_physical(): jnp.einsum('cxtlmy,tlmz->cxyz', along_y, z_table, preferred_element_type=...  48.8 us
  transfers between devices with their start and end apart: 8, of which 2 were waited for; matrix products, arithmetic and copies ran while one was open for 85% of the time, Pallas kernels for 0%

commit v1 on v0

--- a/solution.py
+++ b/solution.py
@@ -1,11 +1,17 @@
+import functools
+import itertools
 import math
 
 import jax
 import jax.numpy as jnp
 from jax import lax
+from jax.experimental import pallas as pl
+from jax.experimental.pallas import tpu as pltpu
 from jax.sharding import PartitionSpec as P
 
+
 PATCH = 4
+VMEM_LIMIT = 66000000
 
 
 NU_DT = 5e-05
@@ -215,9 +221,717 @@
     return (state_grad, grad_in, grad_out, grad_bias)
 
 
+def dot(left, right):
+    return lax.dot_general(
+        left, right, (((1,), (0,)), ((), ())), preferred_element_type=jnp.float32
+    )
+
+
+def dot_t(left, right):
+    return lax.dot_general(
+        left, right, (((1,), (1,)), ((), ())), preferred_element_type=jnp.float32
+    )
+
+
+def spectral_kernel(
+    ids_ref, state_ref, cot_ref, table_ref, *rest, dims, length, ky_count, chunk
+):
+    outs, (rows_ref, wide_ref) = rest[:-2], rest[-2:]
+    width_y, block_z, dests = dims
+    step = pl.program_id(0)
+    cutoff = length // 3
+    half = 2 * width_y
+    halves = length // 128
+    state = state_ref.reshape(6 * width_y * block_z * halves, 128)
+    cot = cot_ref.reshape(6 * width_y * block_z * halves, 128)
+    first_y = ids_ref[0]
+    first_z = ids_ref[1]
+
+    def put(field, row, side, re, im):
+        re = re.astype(jnp.bfloat16)
+        im = im.astype(jnp.bfloat16)
+        base = field // 4 * (4 * half)
+        tile = field % 4
+        for slot, (left, right) in enumerate(((re, im), (im, -re))):
+            place = slot * width_y + row
+            if tile < 3:
+                at = base + tile * 128 + place
+            else:
+                at = base + place // 32 * 128 + half + place % 32
+            rows_ref[at : at + 16, side * 128 : side * 128 + 128] = left
+            rows_ref[at : at + 16, length + side * 128 : length + side * 128 + 128] = right
+
+    def plane(kz, carry):
+        kz_id = first_z + step * block_z + kz
+        start = kz // 8 * (8 * halves) + kz % 8
+        wave_z = jnp.full((1, 1), kz_id, jnp.int32).astype(jnp.float32)
+        keep_z = (wave_z <= cutoff).astype(jnp.float32)
+        weight = jnp.where(wave_z == 0.0, 1.0, 2.0)
+        for row, side in itertools.product(range(0, width_y, 16), range(halves)):
+            lane = side * 128 + lax.broadcasted_iota(jnp.int32, (1, 128), 1)
+            wave_x = jnp.where(lane < length // 2, lane, lane - length).astype(jnp.float32)
+            keep_x = (jnp.abs(wave_x) <= cutoff).astype(jnp.float32)
+            ky_id = first_y + row + lax.broadcasted_iota(jnp.int32, (16, 1), 0)
+            wave_y = jnp.where(ky_id < ky_count // 2, ky_id, ky_id - ky_count).astype(jnp.float32)
+            keep_y = (jnp.abs(wave_y) <= cutoff).astype(jnp.float32)
+            kept = keep_y * keep_z * keep_x
+            square = wave_x * wave_x + (wave_y * wave_y + wave_z * wave_z)
+            damping = jnp.exp(-NU_DT * square)
+            inverse = 1.0 / jnp.maximum(square, 1.0)
+            scale = TIME_STEP * kept * damping
+
+            def load(ref, c, part):
+                at = ((c * 2 + part) * width_y + row) * block_z * halves + side * 8
+                return ref[pl.ds(at + start, 16, stride=block_z * halves), :]
+
+            force = []
+            for part in range(2):
+                v = [load(cot, c, part) for c in range(3)]
+                along = (wave_x * v[0] + wave_y * v[1] + wave_z * v[2]) * inverse
+                force.append(
+                    [scale * (v[c] - k * along) for c, k in enumerate((wave_x, wave_y, wave_z))]
+                )
+            for c in range(3):
+                put(c, row, side, force[0][c], force[1][c])
+            factor = kept * weight
+            for c in range(3):
+                re = factor * load(state, c, 0)
+                im = factor * load(state, c, 1)
+                put(4 + c, row, side, re, im)
+                if c > 0:
+                    put(3 if c == 1 else 7, row, side, -wave_x * im, wave_x * re)
+        lines = dot_t(table_ref[...], rows_ref[...])
+        for tile in range(lines.shape[1] // 128):
+            wide_ref[tile, pl.ds(kz, lines.shape[0], stride=block_z), :] = lines[
+                :, tile * 128 : tile * 128 + 128
+            ]
+        return carry
+
+    lax.fori_loop(0, block_z, plane, 0)
+    slab = table_ref.shape[0] // dests
+    for number, out in enumerate(outs):
+        dest = ids_ref[2] ^ (number % dests)
+        at = (dest * slab + number // dests * chunk) * block_z
+        for x, tile in itertools.product(range(chunk), range(wide_ref.shape[0])):
+            here = pl.ds(pl.multiple_of(at + x * block_z, block_z), block_z)
+            out[x, :, tile * 128 : tile * 128 + 128] = wide_ref[tile, here, :].astype(
+                jnp.bfloat16
+            )
+
+
+def tiled(field):
+    c, parts, width_y, width_z, length = field.shape
+    field = field.reshape(c, parts, width_y, width_z // 8, 8, length // 128, 128)
+    return field.transpose(0, 1, 2, 3, 5, 4, 6)
+
+
+def spectral_stage(ids, state, cotangent, table, dests, ky_count):
+    _, _, width_y, width_z, length = state.shape
+    state, cotangent = tiled(state), tiled(cotangent)
+    chunk, block_z = 8, 16
+    lanes = 16 * width_y
+    block = pl.BlockSpec(
+        (3, 2, width_y, block_z // 8, length // 128, 8, 128),
+        lambda i, s: (0, 0, 0, i, 0, 0, 0),
+    )
+    return pl.pallas_call(
+        functools.partial(
+            spectral_kernel,
+            dims=(width_y, block_z, dests),
+            length=length,
+            ky_count=ky_count,
+            chunk=chunk,
+        ),
+        grid_spec=pltpu.PrefetchScalarGridSpec(
+            num_scalar_prefetch=1,
+            grid=(width_z // block_z,),
+            in_specs=[block, block, pl.BlockSpec(table.shape, lambda i, s: (0, 0))],
+            out_specs=[
+                pl.BlockSpec((chunk, block_z, lanes), lambda i, s: (0, i, 0))
+            ]
+            * (length // chunk),
+            scratch_shapes=[
+                pltpu.VMEM((lanes, 2 * length), jnp.bfloat16),
+                pltpu.VMEM((lanes // 128, length * block_z, 128), jnp.float32),
+            ],
+        ),
+        out_shape=[jax.ShapeDtypeStruct((chunk, width_z, lanes), jnp.bfloat16)]
+        * (length // chunk),
+        compiler_params=pltpu.CompilerParams(vmem_limit_bytes=VMEM_LIMIT),
+        cost_estimate=pl.CostEstimate(
+            flops=2 * length * 2 * length * lanes * width_z,
+            bytes_accessed=60000000,
+            transcendentals=0,
+        ),
+        name="spectral_stage",
+    )(ids, state, cotangent, table)
+
+
+def physical_kernel(*refs, dims):
+    parts_x, parts_y, width_y, width_z, length = dims
+    devices = parts_x * parts_y
+    datas = refs[:devices]
+    out_refs = refs[devices + 14 : 2 * devices + 14]
+    (
+        y_ref,
+        yk_ref,
+        yt_ref,
+        z_ref,
+        zf_ref,
+        yf_ref,
+        kz_ref,
+        ky_ref,
+        w1_ref,
+        w1t_ref,
+        w2t_ref,
+        b_ref,
+        gi_ref,
+        go_ref,
+    ) = refs[devices : devices + 14]
+    (
+        gin_ref,
+        gout_ref,
+        force_ref,
+        vel_ref,
+        vort_ref,
+        adj_ref,
+        line_ref,
+        point_ref,
+        fore_ref,
+        wide_ref,
+        feat_ref,
+        forc_ref,
+        hid_ref,
+        pre_ref,
+    ) = refs[2 * devices + 14 :]
+    group = 8 * width_y
+    rows = 8 * width_z
+    span = parts_y * width_z
+    lane = lax.broadcasted_iota(jnp.int32, (1, 128), 1)
+    low = lane < 64
+
+    def source(py, lanes):
+        return jnp.concatenate(
+            [datas[px * parts_y + py][:, lanes] for px in range(parts_x)], axis=1
+        )
+
+    def tile_of(py, field):
+        at = field // 4 * group + field % 4 * 128
+        return source(py, slice(at, at + 128))
+
+    def place(py, values):
+        for dx in range(4):
+            for ri in range(2):
+                for pair in range(length // 128):
+                    cols = slice(ri * length + pair * 128, ri * length + pair * 128 + 128)
+                    near = values[dx * width_z : (dx + 1) * width_z, cols]
+                    far = values[(4 + dx) * width_z : (5 + dx) * width_z, cols]
+                    even = jnp.where(low, near, pltpu.roll(far, 64, 1))
+                    odd = jnp.where(low, pltpu.roll(near, 64, 1), far)
+                    at = dx * 2 * span + (py * 2 + ri) * width_z
+                    cell = pair * 256
+                    line_ref[at : at + width_z, cell : cell + 128] = even.astype(jnp.bfloat16)
+                    line_ref[at : at + width_z, cell + 128 : cell + 256] = odd.astype(
+                        jnp.bfloat16
+                    )
+
+    def finish(target, c):
+        for dx in range(4):
+            at = (c * 4 + dx) * length
+            values = dot(z_ref[...], line_ref[dx * 2 * span : (dx + 1) * 2 * span, :])
+            for dy in range(4):
+                target[dy, at : at + length, :] = values[:, dy * 128 : dy * 128 + 128].astype(
+                    target.dtype
+                )
+
+    for c in range(3):
+        for py in range(parts_y):
+            place(py, dot(tile_of(py, c), y_ref[...]))
+        finish(force_ref, c)
+    for c in range(3):
+        for py in range(parts_y):
+            values = dot(tile_of(py, 4 + c), y_ref[...])
+            at = (c * parts_y + py) * rows
+            for t in range(4):
+                adj_ref[t, at : at + rows, :] = values[:, t * 128 : t * 128 + 128]
+            place(py, values)
+        finish(vel_ref, c)
+
+    def held(c, py):
+        at = (c * parts_y + py) * rows
+        lines = [adj_ref[t, at : at + rows, :] for t in range(4)]
+        return jnp.concatenate(lines[:2], axis=1), jnp.concatenate(lines[2:], axis=1)
+
+    def slope_y(py, c):
+        lines = tile_of(py, 4 + c)
+        return dot(lines, yk_ref[0]) + dot(lines, yk_ref[1])
+
+    for c in range(3):
+        for py in range(parts_y):
+            wave_z = kz_ref[py]
+            if c == 0:
+                re, im = held(1, py)
+                values = slope_y(py, 2) - jnp.concatenate([-wave_z * im, wave_z * re], axis=1)
+            elif c == 1:
+                re, im = held(0, py)
+                values = jnp.concatenate([-wave_z * im, wave_z * re], axis=1) - dot(
+                    source(py, slice(group, 2 * group)), yt_ref[...]
+                )
+            else:
+                values = dot(source(py, slice(0, group)), yt_ref[...]) - slope_y(py, 0)
+            place(py, values)
+        finish(vort_ref, c)
+
+    gin_ref[...] = gi_ref[...]
+    gout_ref[...] = go_ref[...]
+    count = w1_ref.shape[1]
+    hidden = w1_ref.shape[0]
+    boxes = feat_ref.shape[1]
+    several = boxes // 128
+    cells = length // 4
+    first = lax.broadcasted_iota(jnp.int32, (16, boxes), 0) == 0
+    feat_ref[count : count + 16, :] = first.astype(jnp.bfloat16)
+
+    def closure(step, carry):
+        for k in range(several):
+            bz = step * several + k
+            for dy in range(4):
+                at = pl.ds(bz, 48, stride=cells)
+                feat_ref[dy * 48 : dy * 48 + 48, k * 128 : k * 128 + 128] = vel_ref[
+                    dy, at, :
+                ].astype(jnp.bfloat16)
+                forc_ref[dy * 48 : dy * 48 + 48, k * 128 : k * 128 + 128] = force_ref[
+                    dy, at, :
+                ].astype(jnp.bfloat16)
+
+        def units(part, inner):
+            at = pl.ds(part * 128, 128)
+            pre = dot(w1_ref[at, :], feat_ref[0:count, :]) + b_ref[at, :]
+            sigma = 0.5 * jnp.tanh(0.5 * pre) + 0.5
+            act = pre * sigma
+            back = dot(w2t_ref[at, :], forc_ref[...])
+            hid_ref[at, :] = act.astype(jnp.bfloat16)
+            pre_ref[at, :] = (back * (FORCING * (sigma + act * (1.0 - sigma)))).astype(
+                jnp.bfloat16
+            )
+            return inner
+
+        lax.fori_loop(0, hidden // 128, units, 0)
+        gin_ref[...] += dot_t(pre_ref[...], feat_ref[...])
+        gout_ref[...] += dot_t(forc_ref[...], hid_ref[...])
+        back = dot(w1t_ref[...], pre_ref[...])
+        for k in range(several):
+            bz = step * several + k
+            for dy in range(4):
+                adj_ref[dy, pl.ds(bz, 48, stride=cells), :] = back[
+                    dy * 48 : dy * 48 + 48, k * 128 : k * 128 + 128
+                ]
+        return carry
+
+    lax.fori_loop(0, cells // several, closure, 0)
+
+    def crossing(dx, carry):
+        def strip(part, inner):
+            here = pl.ds(pl.multiple_of(part * 16, 16), 16)
+
+            def at(c):
+                return pl.ds(pl.multiple_of((c * 4 + dx) * length + part * 16, 16), 16)
+
+            for dy in range(4):
+                cols = slice(dy * 128, dy * 128 + 128)
+
+                def rounded(ref):
+                    return [
+                        ref[dy, at(c), :].astype(jnp.bfloat16).astype(jnp.float32)
+                        for c in range(3)
+                    ]
+
+                force = rounded(force_ref)
+                for c, value in enumerate(cross(force, rounded(vel_ref))):
+                    point_ref[3 + c, here, cols] = value.astype(jnp.bfloat16)
+                for c, value in enumerate(cross(rounded(vort_ref), force)):
+                    point_ref[c, here, cols] = (value + adj_ref[dy, at(c), :]).astype(
+                        jnp.bfloat16
+                    )
+            return inner
+
+        lax.fori_loop(0, length // 16, strip, 0)
+        here = pl.ds(pl.multiple_of(dx * span, 16), span)
+        for f in range(6):
+            lines = dot(zf_ref[...], point_ref[f]).astype(jnp.bfloat16)
+            fore_ref[f, here, 0 : 2 * length] = lines[0:span]
+            fore_ref[f, here, 2 * length : 4 * length] = lines[span : 2 * span]
+        return carry
+
+    lax.fori_loop(0, 4, crossing, 0)
+
+    sign = jnp.where(low, -1.0, 1.0)
+    third = lane < width_y
+    two_thirds = lane < 2 * width_y
+
+    def backward(px):
+        wave_y = ky_ref[px, 0:1, :]
+        for pair in range(2):
+            cols = slice(pair * 128, pair * 128 + 128)
+            for dx in range(4):
+                tops = slice(dx * span, (dx + 1) * span)
+                u = [dot(fore_ref[f, tops, :], yf_ref[px, :, cols]) for f in range(6)]
+                for py in range(parts_y):
+                    part = slice(py * width_z, (py + 1) * width_z)
+                    vel = [u[c][part] for c in range(3)]
+                    vort = [u[3 + c][part] for c in range(3)]
+                    wave_z = kz_ref[py, 0:width_z]
+                    turned = sign * pltpu.roll(vort[0], 64, 1)
+                    fields = [
+                        vel[0]
+                        + sign * pltpu.roll(wave_y * vort[2] - wave_z * vort[1], 64, 1),
+                        vel[1] + wave_z * turned,
+                        vel[2] - wave_y * turned,
+                        vort[2],
+                        vort[1],
+                    ]
+                    for ri in range(2):
+                        back = 64 * ri
+
+                        def moved(value, to):
+                            shift = (to - back) % 128
+                            return pltpu.roll(value, shift, 1) if shift else value
+
+                        tail = jnp.where(
+                            two_thirds,
+                            jnp.where(
+                                third, moved(fields[0], 0), moved(fields[1], width_y)
+                            ),
+                            moved(fields[4], 2 * width_y),
+                        )
+                        head = jnp.where(
+                            two_thirds,
+                            jnp.where(
+                                third, moved(fields[2], 0), moved(fields[3], width_y)
+                            ),
+                            moved(fields[4], 2 * width_y - 32),
+                        )
+                        at = py * 16 * width_z + ri * 8 + pair * 4 + dx
+                        wide_ref[0, pl.ds(at, width_z, stride=16), :] = tail
+                        wide_ref[1, pl.ds(at, width_z, stride=16), :] = head
+        for py in range(parts_y):
+            for t in range(2):
+                out_refs[px * parts_y + py][:, t * 128 : t * 128 + 128] = wide_ref[
+                    t, py * 16 * width_z : (py + 1) * 16 * width_z, :
+                ].astype(jnp.bfloat16)
+
+    for px in range(parts_x):
+        backward(px)
+
+
+def physical_stage(data, tables, weights, sums, dims):
+    parts_x, parts_y, _, width_z, length = dims
+    hidden, count = weights[0].shape
+    devices = parts_x * parts_y
+    span = parts_y * width_z
+    vmem = pl.BlockSpec(memory_space=pltpu.VMEM)
+    operands = (*data, *tables, *weights, *sums)
+    cells = 12 * length
+    boxes = 512
+    return pl.pallas_call(
+        functools.partial(physical_kernel, dims=dims),
+        in_specs=[vmem] * len(operands),
+        out_specs=[vmem] * (devices + 2),
+        out_shape=[
+            *[jax.ShapeDtypeStruct((16 * width_z, 256), jnp.bfloat16)] * devices,
+            jax.ShapeDtypeStruct(sums[0].shape, jnp.float32),
+            jax.ShapeDtypeStruct(sums[1].shape, jnp.float32),
+        ],
+        scratch_shapes=[
+            pltpu.VMEM((4, cells, 128), jnp.float32),
+            pltpu.VMEM((4, cells, 128), jnp.float32),
+            pltpu.VMEM((4, cells, 128), jnp.bfloat16),
+            pltpu.VMEM((4, cells, 128), jnp.float32),
+            pltpu.VMEM((4 * 2 * span, 512), jnp.bfloat16),
+            pltpu.VMEM((6, length, 512), jnp.bfloat16),
+            pltpu.VMEM((6, 4 * span, 4 * length), jnp.bfloat16),
+            pltpu.VMEM((2, parts_y * 16 * width_z, 128), jnp.float32),
+            pltpu.VMEM((count + 16, boxes), jnp.bfloat16),
+            pltpu.VMEM((count, boxes), jnp.bfloat16),
+            pltpu.VMEM((hidden, boxes), jnp.bfloat16),
+            pltpu.VMEM((hidden, boxes), jnp.bfloat16),
+        ],
+        compiler_params=pltpu.CompilerParams(vmem_limit_bytes=VMEM_LIMIT),
+        cost_estimate=pl.CostEstimate(
+            flops=40000000000, bytes_accessed=20000000, transcendentals=0
+        ),
+        name="physical_stage",
+    )(*operands)
+
+
+def final_kernel(
+    ids_ref, *rest, width_y, block_z, length, ky_count, chunks
+):
+    datas = rest[:chunks]
+    cot_ref, eye_ref, table_ref, out_ref = rest[chunks:]
+    step = pl.program_id(0)
+    cutoff = length // 3
+    halves = length // 128
+    cot = cot_ref.reshape(6 * width_y * block_z * halves, 128)
+    out = out_ref.reshape(6 * width_y * block_z * halves, 128)
+    first_y = ids_ref[0]
+    first_z = ids_ref[1]
+
+    def plane(kz, carry):
+        kz_id = first_z + step * block_z + kz
+        wave_z = jnp.full((1, 1), kz_id, jnp.int32).astype(jnp.float32)
+        keep_z = (wave_z <= cutoff).astype(jnp.float32)
+        weight = jnp.where(wave_z == 0.0, 1.0, 2.0)
+        here = pl.ds(pl.multiple_of(kz * 16, 16), 16)
+        lines = jnp.concatenate(
+            [data[here, :] for data in datas], axis=0
+        )
+        turned = dot_t(eye_ref[...], lines).astype(jnp.bfloat16)
+        modes = dot(turned, table_ref[...])
+        for row, side in itertools.product(range(0, width_y, 16), range(halves)):
+            lane = side * 128 + lax.broadcasted_iota(jnp.int32, (1, 128), 1)
+            wave_x = jnp.where(lane < length // 2, lane, lane - length).astype(jnp.float32)
+            keep_x = (jnp.abs(wave_x) <= cutoff).astype(jnp.float32)
+            ky_id = first_y + row + lax.broadcasted_iota(jnp.int32, (16, 1), 0)
+            wave_y = jnp.where(ky_id < ky_count // 2, ky_id, ky_id - ky_count).astype(jnp.float32)
+            keep_y = (jnp.abs(wave_y) <= cutoff).astype(jnp.float32)
+            factor = keep_y * keep_z * keep_x * weight
+            square = wave_x * wave_x + (wave_y * wave_y + wave_z * wave_z)
+            damping = jnp.exp(-NU_DT * square)
+            starts = [row, width_y + row, 128 + row, 128 + width_y + row]
+            starts.append(2 * width_y + row if row < 32 else 128 + 2 * width_y + row - 32)
+            cols = [part * length + side * 128 for part in range(2)]
+            f = [[modes[at : at + 16, col : col + 128] for col in cols] for at in starts]
+            spectra = [
+                f[0],
+                [f[1][0] + wave_x * f[3][1], f[1][1] - wave_x * f[3][0]],
+                [f[2][0] - wave_x * f[4][1], f[2][1] + wave_x * f[4][0]],
+            ]
+            for c, part in itertools.product(range(3), range(2)):
+                at = ((c * 2 + part) * width_y + row) * block_z * halves + side * 8
+                where = pl.ds(at + kz, 16, stride=block_z * halves)
+                out[where, :] = damping * cot[where, :] + factor * spectra[c][part]
+        return carry
+
+    lax.fori_loop(0, block_z, plane, 0)
+
+
+def final_stage(ids, datas, cotangent, eye, table, ky_count):
+    shape = cotangent.shape
+    _, _, width_y, width_z, length = shape
+    cotangent = tiled(cotangent)
+    block_z = 8
+    block = pl.BlockSpec(
+        (3, 2, width_y, block_z // 8, length // 128, 8, 128),
+        lambda i, s: (0, 0, 0, i, 0, 0, 0),
+    )
+    result = pl.pallas_call(
+        functools.partial(
+            final_kernel,
+            width_y=width_y,
+            block_z=block_z,
+            length=length,
+            ky_count=ky_count,
+            chunks=len(datas),
+        ),
+        grid_spec=pltpu.PrefetchScalarGridSpec(
+            num_scalar_prefetch=1,
+            grid=(width_z // block_z,),
+            in_specs=[
+                pl.BlockSpec((16 * block_z, d.shape[1]), lambda i, s: (i, 0))
+                for d in datas
+            ]
+            + [
+                block,
+                pl.BlockSpec(eye.shape, lambda i, s: (0, 0)),
+                pl.BlockSpec(table.shape, lambda i, s: (0, 0)),
+            ],
+            out_specs=block,
+        ),
+        out_shape=jax.ShapeDtypeStruct(cotangent.shape, jnp.float32),
+        compiler_params=pltpu.CompilerParams(vmem_limit_bytes=VMEM_LIMIT),
+        cost_estimate=pl.CostEstimate(
+            flops=2 * 256 * 512 * 512 * width_z, bytes_accessed=50000000, transcendentals=0
+        ),
+        name="final_stage",
+    )(ids, *datas, cotangent, eye, table)
+    return result.transpose(0, 1, 2, 3, 5, 4, 6).reshape(shape)
+
+
+def order_of(length):
+    counter = jnp.arange(length, dtype=jnp.int32)
+    cells = length // PATCH
+    return counter % cells * PATCH + counter // cells
+
+
+def pairs(modes, places, length):
+    cosine, sine_part = angles(modes, places, length)
+    return cosine.astype(jnp.bfloat16), sine_part.astype(jnp.bfloat16)
+
+
+def counted(me, parts, width):
+    others = me ^ jnp.arange(parts, dtype=jnp.int32)
+    return (others[:, None] * width + jnp.arange(width, dtype=jnp.int32)).reshape(-1)
+
+
+def exchange(blocks, devices):
+    moved = [blocks[0]]
+    for k in range(1, devices):
+        order = [(i, i ^ k) for i in range(devices)]
+        moved.append(lax.ppermute(blocks[k], ("px", "py"), order))
+    return moved
+
+
+def fast_tables(dims, me_x, me_y):
+    parts_x, parts_y, width_y, width_z, length = dims
+    ky_count = parts_x * width_y
+    grid = jnp.arange(length, dtype=jnp.int32)
+    order = order_of(length)
+    devices = parts_x * parts_y
+    slab = length // devices
+
+    cos_x, sin_x = pairs(grid, grid, length)
+    enter = jnp.concatenate([cos_x, -sin_x], axis=1)
+
+    ky = counted(me_x, parts_x, width_y)
+    modes = jnp.where(ky < ky_count // 2, ky, ky + length - ky_count)
+    wave_y = signed(ky, ky_count)
+    cos_y, sin_y = pairs(modes, order, length)
+    blocked = lambda t: t.reshape(parts_x, width_y, t.shape[-1])
+    fill = 128 - 2 * width_y
+
+    def lined(top, low):
+        both = jnp.concatenate([blocked(top), blocked(low)], axis=1)
+        return jnp.pad(both, ((0, 0), (0, fill), (0, 0))).reshape(parts_x * 128, -1)
+
+    y_top = jnp.concatenate([cos_y, sin_y], axis=1)
+    y_low = jnp.concatenate([-sin_y, cos_y], axis=1)
+    y_table = lined(y_top, y_low)
+    slope = wave_y[:, None]
+    full = lined(slope * y_low.astype(jnp.float32), -slope * y_top.astype(jnp.float32))
+    high = full.astype(jnp.bfloat16)
+    rest = (full - high.astype(jnp.float32)).astype(jnp.bfloat16)
+    y_slope = jnp.stack([high, rest])
+    both = jnp.concatenate([blocked(y_top), blocked(y_low)], axis=1)
+    both = both.reshape(parts_x, 3, 32, -1)
+    y_split = jnp.pad(both, ((0, 0), (0, 0), (2 * width_y, 0), (0, 0))).reshape(
+        parts_x * 384, -1
+    )
+
+    kz = counted(me_y, parts_y, width_z)
+    cos_z, sin_z = pairs(order, kz, length)
+    split = lambda t: t.reshape(length, parts_y, 1, width_z)
+    z_table = jnp.concatenate([split(cos_z), split(-sin_z)], axis=2).reshape(length, -1)
+    z_fore = jnp.concatenate([cos_z.T, -sin_z.T], axis=0)
+
+    cos_f = blocked(cos_y).transpose(0, 2, 1)
+    sin_f = blocked(sin_y).transpose(0, 2, 1)
+    gap = jnp.zeros((parts_x, length, 64 - width_y), jnp.bfloat16)
+    f_re = jnp.concatenate([cos_f, gap, -sin_f, gap], axis=2)
+    f_im = jnp.concatenate([sin_f, gap, cos_f, gap], axis=2)
+
+    def paired(t):
+        t = t.reshape(parts_x, PATCH, 1, length // PATCH, 128)
+        none = jnp.zeros_like(t)
+        near = jnp.concatenate([t, none], axis=2).reshape(parts_x, 2 * length, 128)
+        far = jnp.concatenate([none, t], axis=2).reshape(parts_x, 2 * length, 128)
+        return jnp.concatenate([near, far], axis=2)
+
+    y_fore = jnp.concatenate([paired(f_re), paired(f_im)], axis=1)
+
+    wave_z = kz.astype(jnp.float32).reshape(parts_y, 1, width_z, 1)
+    wave_z = jnp.broadcast_to(wave_z, (parts_y, 8, width_z, 1)).reshape(parts_y, -1, 1)
+    line = jnp.pad(wave_y.reshape(parts_x, width_y), ((0, 0), (0, 64 - width_y)))
+    wave_y = jnp.broadcast_to(
+        jnp.concatenate([line, line], axis=1)[:, None, :], (parts_x, 8, 128)
+    )
+
+    chunks = slab // 8
+    others = (me_x * parts_y + me_y) ^ jnp.arange(devices, dtype=jnp.int32)
+    places = (
+        others[None, :, None] * slab
+        + jnp.arange(chunks, dtype=jnp.int32)[:, None, None] * 8
+        + jnp.arange(8, dtype=jnp.int32)[None, None, :]
+    ).reshape(-1)
+    cos_l, sin_l = pairs(places, grid, length)
+    top = jnp.concatenate([cos_l, -sin_l], axis=1).reshape(chunks * devices, 1, 8, -1)
+    low = jnp.concatenate([sin_l, cos_l], axis=1).reshape(chunks * devices, 1, 8, -1)
+    leave = jnp.concatenate([top, low], axis=1).reshape(2 * length, 2 * length)
+    eye = jnp.eye(256, dtype=jnp.bfloat16)
+    return (
+        enter,
+        (y_table, y_slope, y_split, z_table, z_fore, y_fore, wave_z, wave_y),
+        leave,
+        eye,
+    )
+
+
+def fast_shards(state, cotangent, w_in, b_in, w_out):
+    parts_x = lax.axis_size("px")
+    parts_y = lax.axis_size("py")
+    _, _, width_y, width_z, length = state.shape
+    hidden, count = w_in.shape
+    devices = parts_x * parts_y
+    dims = (parts_x, parts_y, width_y, width_z, length)
+    ky_count = parts_x * width_y
+    me_x, me_y = lax.axis_index("px"), lax.axis_index("py")
+    ids = jnp.stack([me_x * width_y, me_y * width_z, me_x * parts_y + me_y]).astype(jnp.int32)
+    enter, tables, leave, eye = fast_tables(dims, me_x, me_y)
+    sent = spectral_stage(ids, state, cotangent, enter, devices, ky_count)
+    boxed = (count // PATCH**3, PATCH, PATCH, PATCH)
+
+    def by_row(w):
+        return w.reshape(*boxed, hidden).transpose(2, 0, 1, 3, 4).reshape(count, hidden)
+
+    w1t = by_row(w_in.T)
+    w2 = by_row(w_out)
+    weights = (w1t.T, w1t, w2.T, b_in[:, None])
+    sums = (
+        jnp.zeros((hidden, count + 16), jnp.float32),
+        jnp.zeros((count, hidden), jnp.float32),
+    )
+    returned = []
+    for j in range(0, len(sent), devices):
+        moved = exchange(sent[j : j + devices], devices)
+        moved = [block.reshape(8 * width_z, block.shape[-1]) for block in moved]
+        *blocks, gin, gout = physical_stage(moved, tables, weights, sums, dims)
+        sums = (gin, gout)
+        returned += exchange(blocks, devices)
+    state_grad = final_stage(ids, returned, cotangent, eye, leave, ky_count)
+    total = jnp.concatenate([sums[0], FORCING * sums[1].T], axis=1)
+    total = lax.psum_scatter(total, ("px", "py"), scatter_dimension=0, tiled=True)
+    mixed = (PATCH, count // PATCH**3, PATCH, PATCH)
+
+    def by_box(g):
+        return g.reshape(-1, *mixed).transpose(0, 2, 3, 1, 4).reshape(-1, count)
+
+    grad_in = by_box(total[:, :count])
+    grad_bias = total[:, count][None, :]
+    grad_out = by_box(total[:, count + 16 :]).T
+    return (state_grad, grad_in, grad_out, grad_bias)
+
+
+def choose(state, cotangent, w_in, b_in, w_out):
+    _, _, width_y, width_z, length = state.shape
+    devices = lax.axis_size("px") * lax.axis_size("py")
+    fits = (
+        state.shape[0] == 3
+        and width_y == 48
+        and lax.axis_size("px") == 4
+        and lax.axis_size("py") == 2
+        and width_z % 16 == 0
+        and length == 256
+        and length % (8 * devices) == 0
+        and w_in.shape[1] == 3 * PATCH**3
+        and w_in.shape[0] % 128 == 0
+    )
+    body = fast_shards if fits else shards
+    return body(state, cotangent, w_in, b_in, w_out)
+
+
 def solution(mesh):
     return jax.shard_map(
-        shards,
+        choose,
         mesh=mesh,
         in_specs=(
             P("rep", None, "px", "py", None),

time: 1150 us -> 704 us (0.61); the launches traced: 1130 us -> 696 us
  local copies, waits for them, and re-layouts: 618 us -> 15.6 us
  Pallas kernels: 0 us -> 412 us
  matrix products: 297 us -> 0 us
  waiting for transfers between devices: 46.9 us -> 170 us
  other arithmetic: 115 us -> 23.5 us
  starting transfers between devices: 36 us -> 60.1 us
    reshape x19 -> x8, local copies, waits for them, and re-layouts: 523 us -> 1.99 us  [the longest x7 1.24 us: by_row(): w.reshape(*boxed, hidden).transpose(2, 0, 1, 3, 4).reshape(count, hidden)]
    pallas_call x0 -> x6, Pallas kernels: none -> 412 us  [the longest x4 316 us: physical_stage(): pl.pallas_call(functools.partial(physical_kernel, dims=dims), in_specs=[v...]
    dot_general x17 -> x0, matrix products: 297 us -> none  [the longest x2 55.5 us: to_spectral(): jnp.einsum('crlmxy,rysja->csxjlam', along_z, y_table, preferred_element_t...]
    ppermute x0 -> x56, waiting for transfers between devices: none -> 170 us  [exchange(): moved.append(lax.ppermute(blocks[k], ('px', 'py'), order))]
    ppermute x0 -> x56, starting transfers between devices: none -> 60.1 us  [exchange(): moved.append(lax.ppermute(blocks[k], ('px', 'py'), order))]
    all_to_all x5 -> x0, waiting for transfers between devices: 46.9 us -> none  [the longest x3 33 us: to_physical(): lax.all_to_all(along_x, ('px', 'py'), split_axis=2, concat_axis=3, tiled=...]
    another operation x12 -> x2, other arithmetic: 44.1 us -> 1.68 us  [the longest x1 1.07 us: fast_tables(): y_slope = jnp.stack([high, rest])]
    all_to_all x5 -> x0, local copies, waits for them, and re-layouts: 36.8 us -> none  [the longest x3 29.5 us: to_physical(): lax.all_to_all(along_x, ('px', 'py'), split_axis=2, concat_axis=3, tiled=...]
  transfers between devices with their start and end apart: 8 -> 57, of which waited for: 2 -> 20; matrix products, arithmetic and copies ran while one was open for 85% -> 4% of each run, Pallas kernels for 0% -> 39%
where the time goes in v1:
time: 704 us; the launch traced here: 696 us
  Pallas kernels  412 us (59%)
  waiting for transfers between devices  170 us (24%)
  starting transfers between devices  60.1 us (9%)
  other arithmetic  23.5 us (3%)
  local copies, waits for them, and re-layouts  15.6 us (2%)
  between operations  15 us (2%)
    pallas_call x4, Pallas kernels, physical_stage(): pl.pallas_call(functools.partial(physical_kernel, dims=dims), in_specs=[v...  316 us
    ppermute x56, waiting for transfers between devices, exchange(): moved.append(lax.ppermute(blocks[k], ('px', 'py'), order))  170 us
    pallas_call x1, Pallas kernels, spectral_stage(): pl.pallas_call(functools.partial(spectral_kernel, dims=(width_y, block_z,...  63.9 us
    ppermute x56, starting transfers between devices, exchange(): moved.append(lax.ppermute(blocks[k], ('px', 'py'), order))  60.1 us
    pallas_call x1, Pallas kernels, final_stage(): pl.pallas_call(functools.partial(final_kernel, width_y=width_y, block_z=b...  32.6 us
  transfers between devices with their start and end apart: 57, of which 20 were waited for; matrix products, arithmetic and copies ran while one was open for 4% of the time, Pallas kernels for 39%

profile of v1, /device:TPU:0, one launch (start us, length us, event | category | flops | bytes accessed | tf_op | source)
XLA Modules:
  0.0 696.4 jit_solution(1975452788978098307)
XLA Ops:
  10.5 63.9 %spectral_stage.1 = (bf16[8,48,768]{2,1,0:T(8,128)(2,1)}, bf16[8,48,768]{2,1,0:T(8,128)(2,1)}, bf16[8,48,768]{2,1,0:T(8,128)(2,1)}, bf16[8,48,768]{2,1,0:T(8,128...) custom-call(s32[3]{0:T(128)} %pad_add_fusion.ids_ref, ...), custom_call_target="tpu_custom_call" | custom-call | flops 9663676416 | bytes 60000000 | tf_op jit(solution)/shard_map/spectral_stage/pallas_call | solution.py:337
  74.4 2.5 collective-permute-start.2
  76.9 1.5 collective-permute-start.3
  80.1 1.5 collective-permute-start.6
  85.5 2.1 fusion.31
  88.3 2.7 multiply_convert_fusion
  91.2 2.1 collective-permute-start
  93.4 12.9 %collective-permute-done.4 = bf16[8,48,768]{2,1,0:T(8,128)(2,1)} collective-permute-done((bf16[8,48,768]{2,1,0:T(8,128)(2,1)}, bf16[8,48,768]{2,1,0:T(8,128)(2,1)}, u32[]{:S(2)}, u32[]{:S(2)}) %collective-permute-start.4) | collective-permute-done | bytes 589856 | tf_op jit(solution)/shard_map/ppermute | solution.py:781
  115.3 2.9 collective-permute-done.5
  118.9 11.3 %collective-permute-done.6 = bf16[8,48,768]{2,1,0:T(8,128)(2,1)} collective-permute-done((bf16[8,48,768]{2,1,0:T(8,128)(2,1)}, bf16[8,48,768]{2,1,0:T(8,128)(2,1)}, u32[]{:S(2)}, u32[]{:S(2)}) %collective-permute-start.6) | collective-permute-done | bytes 589856 | tf_op jit(solution)/shard_map/ppermute | solution.py:781
  130.2 1.9 collective-permute-start.16
  132.1 1.5 collective-permute-start.17
  133.9 9.6 %collective-permute-done.14 = bf16[8,48,768]{2,1,0:T(8,128)(2,1)} collective-permute-done((bf16[8,48,768]{2,1,0:T(8,128)(2,1)}, bf16[8,48,768]{2,1,0:T(8,128)(2,1)}, u32[]{:S(2)}, u32[]{:S(2)}) %collective-permute-start.14) | collective-permute-done | bytes 589856 | tf_op jit(solution)/shard_map/ppermute | solution.py:781
  146.4 1.6 maximum_maximum_fusion.refs_13_
  148.0 1.6 collective-permute-start.20
  149.6 18.9 %collective-permute-done.16 = bf16[8,48,768]{2,1,0:T(8,128)(2,1)S(1)} collective-permute-done((bf16[8,48,768]{2,1,0:T(8,128)(2,1)}, bf16[8,48,768]{2,1,0:T(8,128)(2,1)S(1)}, u32[]{:S(2)}, u32[]{:S(2)}) %collective-permute-start.16) | collective-permute-done | bytes 589856 | tf_op jit(solution)/shard_map/ppermute | solution.py:781
  168.5 1.7 collective-permute-start.28
  170.7 2.3 collective-permute-done.19
  176.4 86.8 %physical_stage.4 = (bf16[768,256]{1,0:T(8,128)(2,1)}, bf16[768,256]{1,0:T(8,128)(2,1)}, bf16[768,256]{1,0:T(8,128)(2,1)}, bf16[768,256]{1,0:T(8,128)(2,1)}, bf1...) custom-call(bf16[384,768]{1,0:T(8,128)(2,1)} %bitcast.127, ...), custom_call_target="tpu_custom_call" | custom-call | flops 40000000000 | bytes 20000000 | tf_op jit(solution)/shard_map/physical_stage/pallas_call | solution.py:636
  264.1 1.6 collective-permute-start.33
  267.9 76.1 %physical_stage.5 = (bf16[768,256]{1,0:T(8,128)(2,1)}, bf16[768,256]{1,0:T(8,128)(2,1)}, bf16[768,256]{1,0:T(8,128)(2,1)}, bf16[768,256]{1,0:T(8,128)(2,1)}, bf1...) custom-call(bf16[384,768]{1,0:T(8,128)(2,1)} %bitcast.126, ...), custom_call_target="tpu_custom_call" | custom-call | flops 40000000000 | bytes 20000000 | tf_op jit(solution)/shard_map/physical_stage/pallas_call | solution.py:636
  344.0 1.5 collective-permute-start.44
  348.4 2.1 collective-permute-start.48
  350.5 76.3 %physical_stage.6 = (bf16[768,256]{1,0:T(8,128)(2,1)}, bf16[768,256]{1,0:T(8,128)(2,1)}, bf16[768,256]{1,0:T(8,128)(2,1)}, bf16[768,256]{1,0:T(8,128)(2,1)}, bf1...) custom-call(bf16[384,768]{1,0:T(8,128)(2,1)} %bitcast.125, ...), custom_call_target="tpu_custom_call" | custom-call | flops 40000000000 | bytes 20000000 | tf_op jit(solution)/shard_map/physical_stage/pallas_call | solution.py:636
  426.8 76.4 %physical_stage.7 = (bf16[768,256]{1,0:T(8,128)(2,1)}, bf16[768,256]{1,0:T(8,128)(2,1)}, bf16[768,256]{1,0:T(8,128)(2,1)}, bf16[768,256]{1,0:T(8,128)(2,1)}, bf1...) custom-call(bf16[384,768]{1,0:T(8,128)(2,1)} %bitcast.124, ...), custom_call_target="tpu_custom_call" | custom-call | flops 40000000000 | bytes 20000000 | tf_op jit(solution)/shard_map/physical_stage/pallas_call | solution.py:636
  503.8 1.6 collective-permute-start.51
  507.4 8.1 %collective-permute-done.49.rest_25_ = bf16[768,256]{1,0:T(8,128)(2,1)S(1)} collective-permute-done((bf16[768,256]{1,0:T(8,128)(2,1)}, bf16[768,256]{1,0:T(8,128)(2,1)S(1)}, u32[]{:S(2)}, u32[]{:S(2)}) %collective-permute-start.49) | collective-permute-done | bytes 393248 | tf_op jit(solution)/shard_map/ppermute | solution.py:781
  515.8 1.7 collective-permute-start.55
  517.5 12.4 %collective-permute-done.51.rest_27_ = bf16[768,256]{1,0:T(8,128)(2,1)} collective-permute-done((bf16[768,256]{1,0:T(8,128)(2,1)}, bf16[768,256]{1,0:T(8,128)(2,1)}, u32[]{:S(2)}, u32[]{:S(2)}) %collective-permute-start.51) | collective-permute-done | bytes 393248 | tf_op jit(solution)/shard_map/ppermute | solution.py:781
  534.2 7.6 %collective-permute-done.55.rest_31_ = bf16[768,256]{1,0:T(8,128)(2,1)} collective-permute-done((bf16[768,256]{1,0:T(8,128)(2,1)}, bf16[768,256]{1,0:T(8,128)(2,1)}, u32[]{:S(2)}, u32[]{:S(2)}) %collective-permute-start.55) | collective-permute-done | bytes 393248 | tf_op jit(solution)/shard_map/ppermute | solution.py:781
  541.9 1.5 collective-permute-start.39
  543.4 6.8 collective-permute-done.35.rest_17_
  550.2 2.0 collective-permute-start.40
  552.6 14.9 %collective-permute-done.37.rest_19_ = bf16[768,256]{1,0:T(8,128)(2,1)} collective-permute-done((bf16[768,256]{1,0:T(8,128)(2,1)}, bf16[768,256]{1,0:T(8,128)(2,1)}, u32[]{:S(2)}, u32[]{:S(2)}) %collective-permute-start.37) | collective-permute-done | bytes 393248 | tf_op jit(solution)/shard_map/ppermute | solution.py:781
  569.6 1.7 collective-permute-start.24
  571.5 4.1 collective-permute-done.41.rest_23_
  577.1 8.2 %collective-permute-done.21.rest_9_ = bf16[768,256]{1,0:T(8,128)(2,1)S(1)} collective-permute-done((bf16[768,256]{1,0:T(8,128)(2,1)}, bf16[768,256]{1,0:T(8,128)(2,1)S(1)}, u32[]{:S(2)}, u32[]{:S(2)}) %collective-permute-start.21) | collective-permute-done | bytes 393248 | tf_op jit(solution)/shard_map/ppermute | solution.py:781
  585.9 2.1 collective-permute-start.27
  587.9 13.8 %collective-permute-done.23.rest_11_ = bf16[768,256]{1,0:T(8,128)(2,1)S(1)} collective-permute-done((bf16[768,256]{1,0:T(8,128)(2,1)}, bf16[768,256]{1,0:T(8,128)(2,1)S(1)}, u32[]{:S(2)}, u32[]{:S(2)}) %collective-permute-start.23) | collective-permute-done | bytes 393248 | tf_op jit(solution)/shard_map/ppermute | solution.py:781
  602.9 1.8 collective-permute-start.11
  605.9 2.3 pad_maximum_fusion.1
  611.1 1.5 collective-permute-start.7
  612.6 6.5 collective-permute-done.10.rest_4_
  619.1 8.4 %collective-permute-done.11.rest_5_ = bf16[768,256]{1,0:T(8,128)(2,1)} collective-permute-done((bf16[768,256]{1,0:T(8,128)(2,1)}, bf16[768,256]{1,0:T(8,128)(2,1)}, u32[]{:S(2)}, u32[]{:S(2)}) %collective-permute-start.11) | collective-permute-done | bytes 393248 | tf_op jit(solution)/shard_map/ppermute | solution.py:781
  630.3 7.2 %collective-permute-done.12.rest_6_ = bf16[768,256]{1,0:T(8,128)(2,1)S(1)} collective-permute-done((bf16[768,256]{1,0:T(8,128)(2,1)}, bf16[768,256]{1,0:T(8,128)(2,1)S(1)}, u32[]{:S(2)}, u32[]{:S(2)}) %collective-permute-start.12) | collective-permute-done | bytes 393248 | tf_op jit(solution)/shard_map/ppermute | solution.py:781
  637.6 8.9 %collective-permute-done.13.rest_7_ = bf16[768,256]{1,0:T(8,128)(2,1)S(1)} collective-permute-done((bf16[768,256]{1,0:T(8,128)(2,1)}, bf16[768,256]{1,0:T(8,128)(2,1)S(1)}, u32[]{:S(2)}, u32[]{:S(2)}) %collective-permute-start.13) | collective-permute-done | bytes 393248 | tf_op jit(solution)/shard_map/ppermute | solution.py:781
  647.2 4.4 collective-permute-done.9.rest_3_
  652.4 32.6 %final_stage.1 = f32[3,2,48,6,2,8,128]{6,5,4,3,2,1,0:T(8,128)} custom-call(s32[3]{0:T(128)} %pad_add_fusion.ids_ref, bf16[768,256]{1,0:T(8,128)(2,1)} %get-tuple-element.84.rest_0_, bf16[768,256]{1,0:T(8,128)(2,1)} %copy-done.11, bf16[768,256]{1,0:T(8,128)(2,1)} %copy-done.12, bf16[768,256]{1,0:T(8,128)(2,1)} %copy-done.13, ...), custom_call_target="tpu_custom_call" | custom-call | flops 6442450944 | bytes 50000000 | tf_op jit(solution)/shard_map/final_stage/pallas_call | solution.py:728
  (195 shorter events, 57.8 us)
Async XLA Ops:
  7.2 677.8 %reduce-scatter.2.cloned.1.call-start = ((), (), s32[]{:S(2)}) async-start(), calls=%async_computation.1 | async-start | bytes 1179648 | tf_op jit(solution)/shard_map/reduce_scatter | solution.py:902
  78.4 27.8 %collective-permute-start.4 = (bf16[8,48,768]{2,1,0:T(8,128)(2,1)}, bf16[8,48,768]{2,1,0:T(8,128)(2,1)}, u32[]{:S(2)}, u32[]{:S(2)}) collective-permute-start(bf16[8,48,768]{2,1,0:T(8,128)(2,1)} %get-tuple-element.81), channel_id=1, source_target_pairs={{0,5},{1,4},{2,7},{3,6},{4,1},{5,0},{6,3},{7,2},{8,13},{9,12},{10,... | collective-permute-start | bytes 1769480 | tf_op jit(solution)/shard_map/ppermute | solution.py:781
  79.0 39.1 %collective-permute-start.5 = (bf16[8,48,768]{2,1,0:T(8,128)(2,1)}, bf16[8,48,768]{2,1,0:T(8,128)(2,1)}, u32[]{:S(2)}, u32[]{:S(2)}) collective-permute-start(bf16[8,48,768]{2,1,0:T(8,128)(2,1)} %get-tuple-element.82), channel_id=1, source_target_pairs={{0,6},{1,7},{2,4},{3,5},{4,2},{5,3},{6,0},{7,1},{8,14},{9,15},{10,... | collective-permute-start | bytes 1769480 | tf_op jit(solution)/shard_map/ppermute | solution.py:781
  80.1 50.1 %collective-permute-start.6 = (bf16[8,48,768]{2,1,0:T(8,128)(2,1)}, bf16[8,48,768]{2,1,0:T(8,128)(2,1)}, u32[]{:S(2)}, u32[]{:S(2)}) collective-permute-start(bf16[8,48,768]{2,1,0:T(8,128)(2,1)} %get-tuple-element.83), channel_id=1, source_target_pairs={{0,7},{1,6},{2,5},{3,4},{4,3},{5,2},{6,1},{7,0},{8,15},{9,14},{10,... | collective-permute-start | bytes 1769480 | tf_op jit(solution)/shard_map/ppermute | solution.py:781
  91.2 40.9 %collective-permute-start = (bf16[8,48,768]{2,1,0:T(8,128)(2,1)}, bf16[8,48,768]{2,1,0:T(8,128)(2,1)}, u32[]{:S(2)}, u32[]{:S(2)}) collective-permute-start(bf16[8,48,768]{2,1,0:T(8,128)(2,1)} %get-tuple-element.77), channel_id=1, source_target_pairs={{0,1},{1,0},{2,3},{3,2},{4,5},{5,4},{6,7},{7,6},{8,9},{9,8},{10,11... | collective-permute-start | bytes 1769480 | tf_op jit(solution)/shard_map/ppermute | solution.py:781
  93.3 40.3 %collective-permute-start.1 = (bf16[8,48,768]{2,1,0:T(8,128)(2,1)}, bf16[8,48,768]{2,1,0:T(8,128)(2,1)}, u32[]{:S(2)}, u32[]{:S(2)}) collective-permute-start(bf16[8,48,768]{2,1,0:T(8,128)(2,1)} %get-tuple-element.78), channel_id=1, source_target_pairs={{0,2},{1,3},{2,0},{3,1},{4,6},{5,7},{6,4},{7,5},{8,10},{9,11},{10,... | collective-permute-start | bytes 1769480 | tf_op jit(solution)/shard_map/ppermute | solution.py:781
  106.2 37.2 %collective-permute-start.14 = (bf16[8,48,768]{2,1,0:T(8,128)(2,1)}, bf16[8,48,768]{2,1,0:T(8,128)(2,1)}, u32[]{:S(2)}, u32[]{:S(2)}) collective-permute-start(bf16[8,48,768]{2,1,0:T(8,128)(2,1)} %get-tuple-element.93), channel_id=1, source_target_pairs={{0,1},{1,0},{2,3},{3,2},{4,5},{5,4},{6,7},{7,6},{8,9},{9,8},{10,11... | collective-permute-start | bytes 1769480 | tf_op jit(solution)/shard_map/ppermute | solution.py:781
  118.2 29.8 %collective-permute-start.15 = (bf16[8,48,768]{2,1,0:T(8,128)(2,1)}, bf16[8,48,768]{2,1,0:T(8,128)(2,1)S(1)}, u32[]{:S(2)}, u32[]{:S(2)}) collective-permute-start(bf16[8,48,768]{2,1,0:T(8,128)(2,1)} %get-tuple-element.94), channel_id=1, source_target_pairs={{0,2},{1,3},{2,0},{3,1},{4,6},{5,7},{6,4},{7,5},{8,10},{9,11},{10,... | collective-permute-start | bytes 1769480 | tf_op jit(solution)/shard_map/ppermute | solution.py:781
  130.2 38.3 %collective-permute-start.16 = (bf16[8,48,768]{2,1,0:T(8,128)(2,1)}, bf16[8,48,768]{2,1,0:T(8,128)(2,1)S(1)}, u32[]{:S(2)}, u32[]{:S(2)}) collective-permute-start(bf16[8,48,768]{2,1,0:T(8,128)(2,1)} %get-tuple-element.95), channel_id=1, source_target_pairs={{0,3},{1,2},{2,1},{3,0},{4,7},{5,6},{6,5},{7,4},{8,11},{9,10},{10,... | collective-permute-start | bytes 1769480 | tf_op jit(solution)/shard_map/ppermute | solution.py:781
  132.1 38.2 %collective-permute-start.17 = (bf16[8,48,768]{2,1,0:T(8,128)(2,1)}, bf16[8,48,768]{2,1,0:T(8,128)(2,1)S(1)}, u32[]{:S(2)}, u32[]{:S(2)}) collective-permute-start(bf16[8,48,768]{2,1,0:T(8,128)(2,1)} %get-tuple-element.96), channel_id=1, source_target_pairs={{0,4},{1,5},{2,6},{3,7},{4,0},{5,1},{6,2},{7,3},{8,12},{9,13},{10,... | collective-permute-start | bytes 1769480 | tf_op jit(solution)/shard_map/ppermute | solution.py:781
  133.6 36.7 %collective-permute-start.18 = (bf16[8,48,768]{2,1,0:T(8,128)(2,1)}, bf16[8,48,768]{2,1,0:T(8,128)(2,1)S(1)}, u32[]{:S(2)}, u32[]{:S(2)}) collective-permute-start(bf16[8,48,768]{2,1,0:T(8,128)(2,1)} %get-tuple-element.97), channel_id=1, source_target_pairs={{0,5},{1,4},{2,7},{3,6},{4,1},{5,0},{6,3},{7,2},{8,13},{9,12},{10,... | collective-permute-start | bytes 1769480 | tf_op jit(solution)/shard_map/ppermute | solution.py:781
  143.5 29.5 %collective-permute-start.19 = (bf16[8,48,768]{2,1,0:T(8,128)(2,1)}, bf16[8,48,768]{2,1,0:T(8,128)(2,1)S(1)}, u32[]{:S(2)}, u32[]{:S(2)}) collective-permute-start(bf16[8,48,768]{2,1,0:T(8,128)(2,1)} %get-tuple-element.98), channel_id=1, source_target_pairs={{0,6},{1,7},{2,4},{3,5},{4,2},{5,3},{6,0},{7,1},{8,14},{9,15},{10,... | collective-permute-start | bytes 1769480 | tf_op jit(solution)/shard_map/ppermute | solution.py:781
  148.0 115.3 %collective-permute-start.20 = (bf16[8,48,768]{2,1,0:T(8,128)(2,1)}, bf16[8,48,768]{2,1,0:T(8,128)(2,1)}, u32[]{:S(2)}, u32[]{:S(2)}) collective-permute-start(bf16[8,48,768]{2,1,0:T(8,128)(2,1)} %get-tuple-element.99), channel_id=1, source_target_pairs={{0,7},{1,6},{2,5},{3,4},{4,3},{5,2},{6,1},{7,0},{8,15},{9,14},{10,... | collective-permute-start | bytes 1769480 | tf_op jit(solution)/shard_map/ppermute | solution.py:781
  168.5 95.5 %collective-permute-start.28 = (bf16[8,48,768]{2,1,0:T(8,128)(2,1)}, bf16[8,48,768]{2,1,0:T(8,128)(2,1)}, u32[]{:S(2)}, u32[]{:S(2)}) collective-permute-start(bf16[8,48,768]{2,1,0:T(8,128)(2,1)} %get-tuple-element.111), channel_id=1, source_target_pairs={{0,1},{1,0},{2,3},{3,2},{4,5},{5,4},{6,7},{7,6},{8,9},{9,8},{10,11... | collective-permute-start | bytes 1769480 | tf_op jit(solution)/shard_map/ppermute | solution.py:781
  170.3 95.4 %collective-permute-start.29 = (bf16[8,48,768]{2,1,0:T(8,128)(2,1)}, bf16[8,48,768]{2,1,0:T(8,128)(2,1)}, u32[]{:S(2)}, u32[]{:S(2)}) collective-permute-start(bf16[8,48,768]{2,1,0:T(8,128)(2,1)} %get-tuple-element.112), channel_id=1, source_target_pairs={{0,2},{1,3},{2,0},{3,1},{4,6},{5,7},{6,4},{7,5},{8,10},{9,11},{10,... | collective-permute-start | bytes 1769480 | tf_op jit(solution)/shard_map/ppermute | solution.py:781
  170.3 96.5 %collective-permute-start.30 = (bf16[8,48,768]{2,1,0:T(8,128)(2,1)}, bf16[8,48,768]{2,1,0:T(8,128)(2,1)}, u32[]{:S(2)}, u32[]{:S(2)}) collective-permute-start(bf16[8,48,768]{2,1,0:T(8,128)(2,1)} %get-tuple-element.113), channel_id=1, source_target_pairs={{0,3},{1,2},{2,1},{3,0},{4,7},{5,6},{6,5},{7,4},{8,11},{9,10},{10,... | collective-permute-start | bytes 1769480 | tf_op jit(solution)/shard_map/ppermute | solution.py:781
  173.0 94.4 %collective-permute-start.31 = (bf16[8,48,768]{2,1,0:T(8,128)(2,1)S(1)}, bf16[8,48,768]{2,1,0:T(8,128)(2,1)}, u32[]{:S(2)}, u32[]{:S(2)}) collective-permute-start(bf16[8,48,768]{2,1,0:T(8,128)(2,1)S(1)} %copy-done.18), channel_id=1, source_target_pairs={{0,4},{1,5},{2,6},{3,7},{4,0},{5,1},{6,2},{7,3},{8,12},{9,13},{10,... | collective-permute-start | bytes 1769480 | tf_op jit(solution)/shard_map/ppermute | solution.py:781
  263.3 80.8 %collective-permute-start.32 = (bf16[8,48,768]{2,1,0:T(8,128)(2,1)}, bf16[8,48,768]{2,1,0:T(8,128)(2,1)}, u32[]{:S(2)}, u32[]{:S(2)}) collective-permute-start(bf16[8,48,768]{2,1,0:T(8,128)(2,1)} %get-tuple-element.115), channel_id=1, source_target_pairs={{0,5},{1,4},{2,7},{3,6},{4,1},{5,0},{6,3},{7,2},{8,13},{9,12},{10,... | collective-permute-start | bytes 1769480 | tf_op jit(solution)/shard_map/ppermute | solution.py:781
  264.1 81.5 %collective-permute-start.33 = (bf16[8,48,768]{2,1,0:T(8,128)(2,1)}, bf16[8,48,768]{2,1,0:T(8,128)(2,1)}, u32[]{:S(2)}, u32[]{:S(2)}) collective-permute-start(bf16[8,48,768]{2,1,0:T(8,128)(2,1)} %get-tuple-element.116), channel_id=1, source_target_pairs={{0,6},{1,7},{2,4},{3,5},{4,2},{5,3},{6,0},{7,1},{8,14},{9,15},{10,... | collective-permute-start | bytes 1769480 | tf_op jit(solution)/shard_map/ppermute | solution.py:781
  265.7 81.1 %collective-permute-start.34 = (bf16[8,48,768]{2,1,0:T(8,128)(2,1)}, bf16[8,48,768]{2,1,0:T(8,128)(2,1)}, u32[]{:S(2)}, u32[]{:S(2)}) collective-permute-start(bf16[8,48,768]{2,1,0:T(8,128)(2,1)} %get-tuple-element.117), channel_id=1, source_target_pairs={{0,7},{1,6},{2,5},{3,4},{4,3},{5,2},{6,1},{7,0},{8,15},{9,14},{10,... | collective-permute-start | bytes 1769480 | tf_op jit(solution)/shard_map/ppermute | solution.py:781
  266.8 80.8 %collective-permute-start.42 = (bf16[8,48,768]{2,1,0:T(8,128)(2,1)}, bf16[8,48,768]{2,1,0:T(8,128)(2,1)}, u32[]{:S(2)}, u32[]{:S(2)}) collective-permute-start(bf16[8,48,768]{2,1,0:T(8,128)(2,1)} %get-tuple-element.129), channel_id=1, source_target_pairs={{0,1},{1,0},{2,3},{3,2},{4,5},{5,4},{6,7},{7,6},{8,9},{9,8},{10,11... | collective-permute-start | bytes 1769480 | tf_op jit(solution)/shard_map/ppermute | solution.py:781
  267.3 81.0 %collective-permute-start.43 = (bf16[8,48,768]{2,1,0:T(8,128)(2,1)}, bf16[8,48,768]{2,1,0:T(8,128)(2,1)}, u32[]{:S(2)}, u32[]{:S(2)}) collective-permute-start(bf16[8,48,768]{2,1,0:T(8,128)(2,1)} %get-tuple-element.130), channel_id=1, source_target_pairs={{0,2},{1,3},{2,0},{3,1},{4,6},{5,7},{6,4},{7,5},{8,10},{9,11},{10,... | collective-permute-start | bytes 1769480 | tf_op jit(solution)/shard_map/ppermute | solution.py:781
  344.0 82.8 %collective-permute-start.44 = (bf16[8,48,768]{2,1,0:T(8,128)(2,1)}, bf16[8,48,768]{2,1,0:T(8,128)(2,1)}, u32[]{:S(2)}, u32[]{:S(2)}) collective-permute-start(bf16[8,48,768]{2,1,0:T(8,128)(2,1)} %get-tuple-element.131), channel_id=1, source_target_pairs={{0,3},{1,2},{2,1},{3,0},{4,7},{5,6},{6,5},{7,4},{8,11},{9,10},{10,... | collective-permute-start | bytes 1769480 | tf_op jit(solution)/shard_map/ppermute | solution.py:781
  345.6 81.2 %collective-permute-start.45 = (bf16[8,48,768]{2,1,0:T(8,128)(2,1)}, bf16[8,48,768]{2,1,0:T(8,128)(2,1)}, u32[]{:S(2)}, u32[]{:S(2)}) collective-permute-start(bf16[8,48,768]{2,1,0:T(8,128)(2,1)} %get-tuple-element.132), channel_id=1, source_target_pairs={{0,4},{1,5},{2,6},{3,7},{4,0},{5,1},{6,2},{7,3},{8,12},{9,13},{10,... | collective-permute-start | bytes 1769480 | tf_op jit(solution)/shard_map/ppermute | solution.py:781
  346.8 80.0 %collective-permute-start.46 = (bf16[8,48,768]{2,1,0:T(8,128)(2,1)}, bf16[8,48,768]{2,1,0:T(8,128)(2,1)}, u32[]{:S(2)}, u32[]{:S(2)}) collective-permute-start(bf16[8,48,768]{2,1,0:T(8,128)(2,1)} %get-tuple-element.133), channel_id=1, source_target_pairs={{0,5},{1,4},{2,7},{3,6},{4,1},{5,0},{6,3},{7,2},{8,13},{9,12},{10,... | collective-permute-start | bytes 1769480 | tf_op jit(solution)/shard_map/ppermute | solution.py:781
  347.6 79.2 %collective-permute-start.47 = (bf16[8,48,768]{2,1,0:T(8,128)(2,1)}, bf16[8,48,768]{2,1,0:T(8,128)(2,1)}, u32[]{:S(2)}, u32[]{:S(2)}) collective-permute-start(bf16[8,48,768]{2,1,0:T(8,128)(2,1)} %get-tuple-element.134), channel_id=1, source_target_pairs={{0,6},{1,7},{2,4},{3,5},{4,2},{5,3},{6,0},{7,1},{8,14},{9,15},{10,... | collective-permute-start | bytes 1769480 | tf_op jit(solution)/shard_map/ppermute | solution.py:781
  348.4 78.5 %collective-permute-start.48 = (bf16[8,48,768]{2,1,0:T(8,128)(2,1)S(1)}, bf16[8,48,768]{2,1,0:T(8,128)(2,1)}, u32[]{:S(2)}, u32[]{:S(2)}) collective-permute-start(bf16[8,48,768]{2,1,0:T(8,128)(2,1)S(1)} %copy-done.17), channel_id=1, source_target_pairs={{0,7},{1,6},{2,5},{3,4},{4,3},{5,2},{6,1},{7,0},{8,15},{9,14},{10,... | collective-permute-start | bytes 1769480 | tf_op jit(solution)/shard_map/ppermute | solution.py:781
  503.8 26.1 %collective-permute-start.51 = (bf16[768,256]{1,0:T(8,128)(2,1)}, bf16[768,256]{1,0:T(8,128)(2,1)}, u32[]{:S(2)}, u32[]{:S(2)}) collective-permute-start(bf16[768,256]{1,0:T(8,128)(2,1)} %get-tuple-element.141), channel_id=1, source_target_pairs={{0,3},{1,2},{2,1},{3,0},{4,7},{5,6},{6,5},{7,4},{8,11},{9,10},{10,... | collective-permute-start | bytes 1179656 | tf_op jit(solution)/shard_map/ppermute | solution.py:781
  505.4 25.3 %collective-permute-start.52 = (bf16[768,256]{1,0:T(8,128)(2,1)}, bf16[768,256]{1,0:T(8,128)(2,1)}, u32[]{:S(2)}, u32[]{:S(2)}) collective-permute-start(bf16[768,256]{1,0:T(8,128)(2,1)} %get-tuple-element.142), channel_id=1, source_target_pairs={{0,4},{1,5},{2,6},{3,7},{4,0},{5,1},{6,2},{7,3},{8,12},{9,13},{10,... | collective-permute-start | bytes 1179656 | tf_op jit(solution)/shard_map/ppermute | solution.py:781
  506.7 24.9 %collective-permute-start.53 = (bf16[768,256]{1,0:T(8,128)(2,1)}, bf16[768,256]{1,0:T(8,128)(2,1)}, u32[]{:S(2)}, u32[]{:S(2)}) collective-permute-start(bf16[768,256]{1,0:T(8,128)(2,1)} %get-tuple-element.143), channel_id=1, source_target_pairs={{0,5},{1,4},{2,7},{3,6},{4,1},{5,0},{6,3},{7,2},{8,13},{9,12},{10,... | collective-permute-start | bytes 1179656 | tf_op jit(solution)/shard_map/ppermute | solution.py:781
  515.8 26.1 %collective-permute-start.55 = (bf16[768,256]{1,0:T(8,128)(2,1)}, bf16[768,256]{1,0:T(8,128)(2,1)}, u32[]{:S(2)}, u32[]{:S(2)}) collective-permute-start(bf16[768,256]{1,0:T(8,128)(2,1)} %get-tuple-element.145), channel_id=1, source_target_pairs={{0,7},{1,6},{2,5},{3,4},{4,3},{5,2},{6,1},{7,0},{8,15},{9,14},{10,... | collective-permute-start | bytes 1179656 | tf_op jit(solution)/shard_map/ppermute | solution.py:781
  529.9 20.3 %collective-permute-start.35 = (bf16[768,256]{1,0:T(8,128)(2,1)}, bf16[768,256]{1,0:T(8,128)(2,1)}, u32[]{:S(2)}, u32[]{:S(2)}) collective-permute-start(bf16[768,256]{1,0:T(8,128)(2,1)} %get-tuple-element.121), channel_id=1, source_target_pairs={{0,1},{1,0},{2,3},{3,2},{4,5},{5,4},{6,7},{7,6},{8,9},{9,8},{10,11... | collective-permute-start | bytes 1179656 | tf_op jit(solution)/shard_map/ppermute | solution.py:781
  530.8 21.5 %collective-permute-start.36 = (bf16[768,256]{1,0:T(8,128)(2,1)}, bf16[768,256]{1,0:T(8,128)(2,1)}, u32[]{:S(2)}, u32[]{:S(2)}) collective-permute-start(bf16[768,256]{1,0:T(8,128)(2,1)} %get-tuple-element.122), channel_id=1, source_target_pairs={{0,2},{1,3},{2,0},{3,1},{4,6},{5,7},{6,4},{7,5},{8,10},{9,11},{10,... | collective-permute-start | bytes 1179656 | tf_op jit(solution)/shard_map/ppermute | solution.py:781
  531.6 35.9 %collective-permute-start.37 = (bf16[768,256]{1,0:T(8,128)(2,1)}, bf16[768,256]{1,0:T(8,128)(2,1)}, u32[]{:S(2)}, u32[]{:S(2)}) collective-permute-start(bf16[768,256]{1,0:T(8,128)(2,1)} %get-tuple-element.123), channel_id=1, source_target_pairs={{0,3},{1,2},{2,1},{3,0},{4,7},{5,6},{6,5},{7,4},{8,11},{9,10},{10,... | collective-permute-start | bytes 1179656 | tf_op jit(solution)/shard_map/ppermute | solution.py:781
  533.4 34.8 %collective-permute-start.38 = (bf16[768,256]{1,0:T(8,128)(2,1)}, bf16[768,256]{1,0:T(8,128)(2,1)}, u32[]{:S(2)}, u32[]{:S(2)}) collective-permute-start(bf16[768,256]{1,0:T(8,128)(2,1)} %get-tuple-element.124), channel_id=1, source_target_pairs={{0,4},{1,5},{2,6},{3,7},{4,0},{5,1},{6,2},{7,3},{8,12},{9,13},{10,... | collective-permute-start | bytes 1179656 | tf_op jit(solution)/shard_map/ppermute | solution.py:781
  541.9 26.4 %collective-permute-start.39 = (bf16[768,256]{1,0:T(8,128)(2,1)}, bf16[768,256]{1,0:T(8,128)(2,1)}, u32[]{:S(2)}, u32[]{:S(2)}) collective-permute-start(bf16[768,256]{1,0:T(8,128)(2,1)} %get-tuple-element.125), channel_id=1, source_target_pairs={{0,5},{1,4},{2,7},{3,6},{4,1},{5,0},{6,3},{7,2},{8,13},{9,12},{10,... | collective-permute-start | bytes 1179656 | tf_op jit(solution)/shard_map/ppermute | solution.py:781
  552.3 23.4 %collective-permute-start.41 = (bf16[768,256]{1,0:T(8,128)(2,1)}, bf16[768,256]{1,0:T(8,128)(2,1)S(1)}, u32[]{:S(2)}, u32[]{:S(2)}) collective-permute-start(bf16[768,256]{1,0:T(8,128)(2,1)} %get-tuple-element.127), channel_id=1, source_target_pairs={{0,7},{1,6},{2,5},{3,4},{4,3},{5,2},{6,1},{7,0},{8,15},{9,14},{10,... | collective-permute-start | bytes 1179656 | tf_op jit(solution)/shard_map/ppermute | solution.py:781
  568.3 33.5 %collective-permute-start.23 = (bf16[768,256]{1,0:T(8,128)(2,1)}, bf16[768,256]{1,0:T(8,128)(2,1)S(1)}, u32[]{:S(2)}, u32[]{:S(2)}) collective-permute-start(bf16[768,256]{1,0:T(8,128)(2,1)} %get-tuple-element.105), channel_id=1, source_target_pairs={{0,3},{1,2},{2,1},{3,0},{4,7},{5,6},{6,5},{7,4},{8,11},{9,10},{10,... | collective-permute-start | bytes 1179656 | tf_op jit(solution)/shard_map/ppermute | solution.py:781
  569.6 33.4 %collective-permute-start.24 = (bf16[768,256]{1,0:T(8,128)(2,1)}, bf16[768,256]{1,0:T(8,128)(2,1)S(1)}, u32[]{:S(2)}, u32[]{:S(2)}) collective-permute-start(bf16[768,256]{1,0:T(8,128)(2,1)} %get-tuple-element.106), channel_id=1, source_target_pairs={{0,4},{1,5},{2,6},{3,7},{4,0},{5,1},{6,2},{7,3},{8,12},{9,13},{10,... | collective-permute-start | bytes 1179656 | tf_op jit(solution)/shard_map/ppermute | solution.py:781
  575.7 33.6 %collective-permute-start.25 = (bf16[768,256]{1,0:T(8,128)(2,1)}, bf16[768,256]{1,0:T(8,128)(2,1)S(1)}, u32[]{:S(2)}, u32[]{:S(2)}) collective-permute-start(bf16[768,256]{1,0:T(8,128)(2,1)} %get-tuple-element.107), channel_id=1, source_target_pairs={{0,5},{1,4},{2,7},{3,6},{4,1},{5,0},{6,3},{7,2},{8,13},{9,12},{10,... | collective-permute-start | bytes 1179656 | tf_op jit(solution)/shard_map/ppermute | solution.py:781
  585.3 24.9 %collective-permute-start.26 = (bf16[768,256]{1,0:T(8,128)(2,1)}, bf16[768,256]{1,0:T(8,128)(2,1)}, u32[]{:S(2)}, u32[]{:S(2)}) collective-permute-start(bf16[768,256]{1,0:T(8,128)(2,1)} %get-tuple-element.108), channel_id=1, source_target_pairs={{0,6},{1,7},{2,4},{3,5},{4,2},{5,3},{6,0},{7,1},{8,14},{9,15},{10,... | collective-permute-start | bytes 1179656 | tf_op jit(solution)/shard_map/ppermute | solution.py:781
  585.9 25.3 %collective-permute-start.27 = (bf16[768,256]{1,0:T(8,128)(2,1)}, bf16[768,256]{1,0:T(8,128)(2,1)}, u32[]{:S(2)}, u32[]{:S(2)}) collective-permute-start(bf16[768,256]{1,0:T(8,128)(2,1)} %get-tuple-element.109), channel_id=1, source_target_pairs={{0,7},{1,6},{2,5},{3,4},{4,3},{5,2},{6,1},{7,0},{8,15},{9,14},{10,... | collective-permute-start | bytes 1179656 | tf_op jit(solution)/shard_map/ppermute | solution.py:781
  602.9 24.6 %collective-permute-start.11 = (bf16[768,256]{1,0:T(8,128)(2,1)}, bf16[768,256]{1,0:T(8,128)(2,1)}, u32[]{:S(2)}, u32[]{:S(2)}) collective-permute-start(bf16[768,256]{1,0:T(8,128)(2,1)} %get-tuple-element.89), channel_id=1, source_target_pairs={{0,5},{1,4},{2,7},{3,6},{4,1},{5,0},{6,3},{7,2},{8,13},{9,12},{10,... | collective-permute-start | bytes 1179656 | tf_op jit(solution)/shard_map/ppermute | solution.py:781
  609.4 28.2 %collective-permute-start.12 = (bf16[768,256]{1,0:T(8,128)(2,1)}, bf16[768,256]{1,0:T(8,128)(2,1)S(1)}, u32[]{:S(2)}, u32[]{:S(2)}) collective-permute-start(bf16[768,256]{1,0:T(8,128)(2,1)} %get-tuple-element.90), channel_id=1, source_target_pairs={{0,6},{1,7},{2,4},{3,5},{4,2},{5,3},{6,0},{7,1},{8,14},{9,15},{10,... | collective-permute-start | bytes 1179656 | tf_op jit(solution)/shard_map/ppermute | solution.py:781
  610.1 36.4 %collective-permute-start.13 = (bf16[768,256]{1,0:T(8,128)(2,1)}, bf16[768,256]{1,0:T(8,128)(2,1)S(1)}, u32[]{:S(2)}, u32[]{:S(2)}) collective-permute-start(bf16[768,256]{1,0:T(8,128)(2,1)} %get-tuple-element.91), channel_id=1, source_target_pairs={{0,7},{1,6},{2,5},{3,4},{4,3},{5,2},{6,1},{7,0},{8,15},{9,14},{10,... | collective-permute-start | bytes 1179656 | tf_op jit(solution)/shard_map/ppermute | solution.py:781
  611.1 35.4 %collective-permute-start.7 = (bf16[768,256]{1,0:T(8,128)(2,1)}, bf16[768,256]{1,0:T(8,128)(2,1)S(1)}, u32[]{:S(2)}, u32[]{:S(2)}) collective-permute-start(bf16[768,256]{1,0:T(8,128)(2,1)} %get-tuple-element.85), channel_id=1, source_target_pairs={{0,1},{1,0},{2,3},{3,2},{4,5},{5,4},{6,7},{7,6},{8,9},{9,8},{10,11... | collective-permute-start | bytes 1179656 | tf_op jit(solution)/shard_map/ppermute | solution.py:781
  619.1 27.4 %collective-permute-start.8 = (bf16[768,256]{1,0:T(8,128)(2,1)}, bf16[768,256]{1,0:T(8,128)(2,1)S(1)}, u32[]{:S(2)}, u32[]{:S(2)}) collective-permute-start(bf16[768,256]{1,0:T(8,128)(2,1)} %get-tuple-element.86), channel_id=1, source_target_pairs={{0,2},{1,3},{2,0},{3,1},{4,6},{5,7},{6,4},{7,5},{8,10},{9,11},{10,... | collective-permute-start | bytes 1179656 | tf_op jit(solution)/shard_map/ppermute | solution.py:781
  627.5 24.1 %collective-permute-start.9 = (bf16[768,256]{1,0:T(8,128)(2,1)}, bf16[768,256]{1,0:T(8,128)(2,1)S(1)}, u32[]{:S(2)}, u32[]{:S(2)}) collective-permute-start(bf16[768,256]{1,0:T(8,128)(2,1)} %get-tuple-element.87), channel_id=1, source_target_pairs={{0,3},{1,2},{2,1},{3,0},{4,7},{5,6},{6,5},{7,4},{8,11},{9,10},{10,... | collective-permute-start | bytes 1179656 | tf_op jit(solution)/shard_map/ppermute | solution.py:781
  (35 other events, 899.5 us)
Sparse Core Ops, SparseCore 0:
  608.4 41.6 reduce-scatter.1
